TPU v7x, 32 devices: a whole 2x2x4 slice. The times are simulated.
32 devices in a mesh: dp: 8 (over y, x, core), shard: 4 (over z).
Axes of the slice: x: 2, y: 2, z: 4, core: 2. Of those that a mesh axis runs over, the one named last changes fastest.
Arguments:
- block_input: bfloat16 [16384, 768], P(('dp', 'shard')), may hold values from -64 to 64
- cotangent: bfloat16 [16384, 768], P(('dp', 'shard')), may hold values from -4 to 4
- token_bounds: int32 [32, 2], P(('dp', 'shard')), may hold values from 0 to 11426, as said below
- params: float32 [7087104], P('shard'), may hold values from -3 to 3
- first_moment: float32 [7087104], P('shard')
- second_moment: float32 [7087104], P('shard'), as said below
Outputs:
- activations: float32 [16384, 768], P(('dp', 'shard'))
- input_grad: float32 [16384, 768], P(('dp', 'shard'))
- param_grad: float32 [4, 8, 221472], P('shard', 'dp')
- new_params: float32 [7087104], P('shard')
- new_first: float32 [7087104], P('shard')
- new_second: float32 [7087104], P('shard')
Inputs may be any that keep to these rules, and one draw needn't show every extreme that they name: `token_bounds`: row d, devices taken in the order of dp then shard, holds the first token and one past the last token of device d among the 11426 tokens in image order. The ranges meet end to start, the first begins at 0 and the last ends at 11426. Every device holds at least 197 and at most 512 tokens, and some device exactly 512. `second_moment`: every entry is positive.
All inputs are finite; a program needn't handle non-finite values.
Results may differ from a plain program's by a relative error of at most 0.02.
The roundings to bfloat16 on the way count: a program that leaves them out, or rounds other values in their place, can miss the bound.
Values may be sent and summed in bfloat16 or wider, within the bound.
A program may use at most 256 MiB of HBM per device.

v0:
```python
import jax
import jax.numpy as jnp
from jax import lax
from jax.sharding import PartitionSpec as P

D = 768
HEADS = 12
HD = 64
FF = 3072
IMG = 197
BLOCK = 512
HALO = 196
KEY_SPAN = 1024


ln_eps = 1e-06
masked = -1e30
beta_one = 0.9
beta_two = 0.999
learn_rate = 0.02
decay_rate = 0.05
adam_eps = 1e-08
sqrt_half = 0.7071067811865476
inv_root_two_pi = 0.3989422804014327


def extended_2(cells, sides, width):
    for axis, dim in sides:
        count = lax.axis_size(axis)
        ends = count - 1
        head = lax.slice_in_dim(cells, 0, width, axis=dim)
        tail = lax.slice_in_dim(cells, cells.shape[dim] - width, cells.shape[dim], axis=dim)
        cells = jnp.concatenate(
            [
                lax.ppermute(tail, axis, [(i, (i + 1) % count) for i in range(ends)]),
                cells,
                lax.ppermute(head, axis, [((i + 1) % count, i) for i in range(ends)]),
            ],
            axis=dim,
        )
    return cells


def gelu_value(preact):
    return 0.5 * preact * (1.0 + lax.erf(preact * sqrt_half))


def gelu_slope(preact):
    return (
        0.5 * (1.0 + lax.erf(preact * sqrt_half))
        + preact * jnp.exp(-0.5 * preact * preact) * inv_root_two_pi
    )


def norm_forward(values, gain_vec, shift_vec):
    centre = jnp.mean(values, axis=-1, keepdims=True)
    centred = values - centre
    spread = jnp.mean(centred * centred, axis=-1, keepdims=True)
    inverse = lax.rsqrt(spread + ln_eps)
    normed = centred * inverse
    return (normed * gain_vec + shift_vec, normed, inverse)


def norm_backward(upstream, normed, inverse, gain_vec):
    scaled = upstream * gain_vec
    first_mean = jnp.mean(scaled, axis=-1, keepdims=True)
    second = jnp.mean(scaled * normed, axis=-1, keepdims=True)
    return inverse * (scaled - first_mean - normed * second)


def unpack(flat_vec):
    lengths = [3 * D * D, D * D, D * FF, FF * D, 8 * D, FF]
    pieces = []
    cursor = 0
    for extent in lengths:
        pieces.append(flat_vec[cursor : cursor + extent])
        cursor = cursor + extent
    return (
        pieces[0].reshape(D, 3 * D),
        pieces[1].reshape(D, D),
        pieces[2].reshape(D, FF),
        pieces[3].reshape(FF, D),
        pieces[4].reshape(8, D),
        pieces[5],
    )


def split_heads(matrix):
    return matrix.reshape(matrix.shape[0], HEADS, HD)


def block_scores(query_rows, key_rows, allowed):
    raw = jnp.einsum(
        "qhd,khd->hqk",
        split_heads(query_rows),
        split_heads(key_rows),
        preferred_element_type=jnp.float32,
    )
    return jnp.where(allowed[None], raw, masked)


def shards(block_input, cotangent, token_bounds, params, first_moment, second_moment):
    rows_here = block_input.shape[0]
    own_len = params.shape[0]
    gathered = lax.all_gather(params.astype(jnp.bfloat16), "shard", axis=0, tiled=True)
    weight_qkv, weight_out, weight_in, weight_back, vectors, bias_raw = unpack(gathered)
    vector_f = vectors.astype(jnp.float32)
    bias_in = bias_raw.astype(jnp.float32)
    gain_one, shift_one, bias_q, bias_v = (vector_f[0], vector_f[1], vector_f[2], vector_f[3])
    bias_out, gain_two, shift_two, bias_back = (vector_f[4], vector_f[5], vector_f[6], vector_f[7])
    start_tok = token_bounds[0, 0]
    stop_tok = token_bounds[0, 1]
    live_count = stop_tok - start_tok
    slot_ids = jnp.arange(rows_here, dtype=jnp.int32)
    is_live = slot_ids < live_count
    positions = start_tok + slot_ids
    stream = block_input.astype(jnp.float32)
    first_out, first_normed, first_inv = norm_forward(stream, gain_one, shift_one)
    first_feed = first_out.astype(jnp.bfloat16)
    projected = jnp.dot(first_feed, weight_qkv, preferred_element_type=jnp.float32)
    queries = ((projected[:, :D] + bias_q) * 0.125).astype(jnp.bfloat16)
    key_value = jnp.concatenate(
        [projected[:, D : 2 * D], projected[:, 2 * D :] + bias_v], axis=1
    ).astype(jnp.bfloat16)
    rim_rows = jnp.concatenate(
        [key_value[:HALO], lax.dynamic_slice_in_dim(key_value, live_count - HALO, HALO, 0)], axis=0
    )
    rim_pairs = extended_2(rim_rows, ((("dp", "shard"), 0),), HALO)
    spare_rows = KEY_SPAN - BLOCK - 2 * HALO
    extended = jnp.concatenate(
        [
            rim_pairs[:HALO],
            key_value,
            rim_pairs[3 * HALO :],
            jnp.zeros((spare_rows, 2 * D), jnp.bfloat16),
        ],
        axis=0,
    )
    cycle_place = lax.axis_index(("dp", "shard"))
    cycle_last = lax.axis_size(("dp", "shard")) - 1
    lane_ids = jnp.arange(HALO, dtype=jnp.int32)
    key_pos = jnp.concatenate(
        [
            start_tok - HALO + lane_ids,
            positions,
            stop_tok + lane_ids,
            jnp.zeros((spare_rows,), jnp.int32),
        ]
    )
    key_ok = jnp.concatenate(
        [
            jnp.broadcast_to(cycle_place > 0, (HALO,)),
            is_live,
            jnp.broadcast_to(cycle_place < cycle_last, (HALO,)),
            jnp.zeros((spare_rows,), jnp.bool_),
        ]
    )
    key_image = jnp.where(key_ok, key_pos // IMG, -1)
    query_image = positions // IMG

    def block_view(head_row):
        allowed = (
            query_image[head_row : head_row + BLOCK, None]
            == key_image[None, head_row : head_row + KEY_SPAN]
        )
        return (allowed, extended)

    block_num = 0
    head_row = block_num * BLOCK
    allowed, key_part = block_view(head_row)
    scores = block_scores(queries, key_part[:, :D], allowed)
    row_top = jnp.max(scores, axis=-1, keepdims=True)
    log_total = row_top + jnp.log(jnp.sum(jnp.exp(scores - row_top), axis=-1, keepdims=True))
    probs_b = jnp.exp(scores - log_total).astype(jnp.bfloat16)
    block_out = jnp.einsum(
        "hqk,khd->qhd", probs_b, split_heads(key_part[:, D:]), preferred_element_type=jnp.float32
    )
    attended_list = block_out.reshape(BLOCK, D).astype(jnp.bfloat16)
    lse_list = [log_total]
    middle = (
        stream + jnp.dot(attended_list, weight_out, preferred_element_type=jnp.float32) + bias_out
    )
    second_out, second_normed, second_inv = norm_forward(middle, gain_two, shift_two)
    second_feed = second_out.astype(jnp.bfloat16)
    preact = jnp.dot(second_feed, weight_in, preferred_element_type=jnp.float32) + bias_in
    activated = gelu_value(preact).astype(jnp.bfloat16)
    result = (
        middle + jnp.dot(activated, weight_back, preferred_element_type=jnp.float32) + bias_back
    )
    activations = jnp.where(is_live[:, None], result, 0.0)
    tangent_b = jnp.where(is_live[:, None], cotangent, jnp.zeros_like(cotangent))
    tangent = tangent_b.astype(jnp.float32)
    grad_back = jnp.einsum("tf,td->fd", activated, tangent_b, preferred_element_type=jnp.float32)
    grad_bias_back = jnp.sum(tangent, axis=0)
    slope_in = jnp.einsum(
        "td,fd->tf", tangent_b, weight_back, preferred_element_type=jnp.float32
    ) * gelu_slope(preact)
    grad_bias_in = jnp.sum(slope_in, axis=0)
    slope_feed = slope_in.astype(jnp.bfloat16)
    grad_in = jnp.einsum("td,tf->df", second_feed, slope_feed, preferred_element_type=jnp.float32)
    back_two = jnp.einsum("tf,df->td", slope_feed, weight_in, preferred_element_type=jnp.float32)
    grad_gain_two = jnp.sum(back_two * second_normed, axis=0)
    grad_shift_two = jnp.sum(back_two, axis=0)
    middle_grad = tangent + norm_backward(back_two, second_normed, second_inv, gain_two)
    middle_feed = middle_grad.astype(jnp.bfloat16)
    grad_out = jnp.einsum(
        "td,te->de", attended_list, middle_feed, preferred_element_type=jnp.float32
    )
    grad_bias_out = jnp.sum(middle_grad, axis=0)
    attended_grad = jnp.einsum(
        "te,de->td", middle_feed, weight_out, preferred_element_type=jnp.float32
    ).astype(jnp.bfloat16)
    ext_grad = jnp.zeros((rows_here + KEY_SPAN - BLOCK, 2 * D), jnp.float32)
    block_num = 0
    head_row = block_num * BLOCK
    allowed, key_part = block_view(head_row)
    scores = block_scores(queries, key_part[:, :D], allowed)
    probs_f = jnp.exp(scores - lse_list[block_num])
    probs_b = probs_f.astype(jnp.bfloat16)
    grad_part = split_heads(attended_grad)
    value_part = split_heads(key_part[:, D:])
    value_grad = jnp.einsum("hqk,qhd->khd", probs_b, grad_part, preferred_element_type=jnp.float32)
    prob_grad = jnp.einsum(
        "qhd,khd->hqk", grad_part, value_part, preferred_element_type=jnp.float32
    )
    centre_term = jnp.sum(
        grad_part.astype(jnp.float32) * split_heads(attended_list).astype(jnp.float32), axis=-1
    )
    score_grad = (probs_f * (prob_grad - jnp.transpose(centre_term)[:, :, None])).astype(
        jnp.bfloat16
    )
    block_qgrad = jnp.einsum(
        "hqk,khd->qhd", score_grad, split_heads(key_part[:, :D]), preferred_element_type=jnp.float32
    )
    query_grads = block_qgrad.reshape(BLOCK, D) * 0.125
    key_grad = jnp.einsum(
        "hqk,qhd->khd", score_grad, split_heads(queries), preferred_element_type=jnp.float32
    )
    ext_grad = ext_grad.at[head_row : head_row + KEY_SPAN].add(
        jnp.concatenate([key_grad.reshape(KEY_SPAN, D), value_grad.reshape(KEY_SPAN, D)], axis=1)
    )
    outgoing = jnp.concatenate(
        [ext_grad[:HALO], ext_grad[HALO + rows_here : 2 * HALO + rows_here]], axis=0
    )
    incoming = extended_2(outgoing, ((("dp", "shard"), 0),), HALO)
    own_grad = ext_grad[HALO : HALO + rows_here]
    own_grad = own_grad.at[:HALO].add(incoming[:HALO])
    tail_now = lax.dynamic_slice_in_dim(own_grad, live_count - HALO, HALO, 0)
    own_grad = lax.dynamic_update_slice_in_dim(
        own_grad, tail_now + incoming[3 * HALO :], live_count - HALO, 0
    )
    grad_bias_q = jnp.sum(query_grads, axis=0)
    grad_bias_v = jnp.sum(own_grad[:, D:], axis=0)
    joined = jnp.concatenate([query_grads, own_grad], axis=1).astype(jnp.bfloat16)
    grad_qkv = jnp.einsum("td,te->de", first_feed, joined, preferred_element_type=jnp.float32)
    back_one = jnp.einsum("te,de->td", joined, weight_qkv, preferred_element_type=jnp.float32)
    grad_gain_one = jnp.sum(back_one * first_normed, axis=0)
    grad_shift_one = jnp.sum(back_one, axis=0)
    stream_grad = middle_grad + norm_backward(back_one, first_normed, first_inv, gain_one)
    input_grad = jnp.where(is_live[:, None], stream_grad, 0.0)
    vector_grad = jnp.stack(
        [
            grad_gain_one,
            grad_shift_one,
            grad_bias_q,
            grad_bias_v,
            grad_bias_out,
            grad_gain_two,
            grad_shift_two,
            grad_bias_back,
        ]
    )
    grad_flat = jnp.concatenate(
        [
            grad_qkv.reshape(-1),
            grad_out.reshape(-1),
            grad_in.reshape(-1),
            grad_back.reshape(-1),
            vector_grad.reshape(-1),
            grad_bias_in,
        ]
    )
    piece_len = own_len // lax.axis_size("dp")
    summed = lax.psum(grad_flat, ("dp", "shard"))
    grad_shard = lax.dynamic_slice_in_dim(summed, lax.axis_index("shard") * own_len, own_len, 0)
    grad_piece = lax.dynamic_slice_in_dim(
        grad_shard, lax.axis_index("dp") * piece_len, piece_len, 0
    )
    matrices = 4 * D * D + 2 * D * FF
    global_ids = lax.axis_index("shard") * own_len + jnp.arange(own_len, dtype=jnp.int32)
    decays = (global_ids < matrices).astype(jnp.float32)
    new_first = beta_one * first_moment + (1.0 - beta_one) * grad_shard
    new_second = beta_two * second_moment + (1.0 - beta_two) * grad_shard * grad_shard
    first_hat = new_first / (1.0 - beta_one**3)
    second_hat = new_second / (1.0 - beta_two**3)
    new_params = params - learn_rate * (
        first_hat / (jnp.sqrt(second_hat) + adam_eps) + decay_rate * decays * params
    )
    param_grad = grad_piece.reshape(1, 1, piece_len)
    return (activations, input_grad, param_grad, new_params, new_first, new_second)


def solution(mesh):
    in_specs = (
        P(("dp", "shard"), None),
        P(("dp", "shard"), None),
        P(("dp", "shard"), None),
        P("shard"),
        P("shard"),
        P("shard"),
    )
    out_specs = (
        P(("dp", "shard"), None),
        P(("dp", "shard"), None),
        P("shard", "dp", None),
        P("shard"),
        P("shard"),
        P("shard"),
    )
    return jax.shard_map(shards, mesh=mesh, in_specs=in_specs, out_specs=out_specs, check_vma=False)
```

profile of v0, /device:TPU:1, one launch (start us, length us, event | category | flops | bytes accessed | tf_op | source)
XLA Modules:
  0.0 1400.9 jit_solution(12401584358553554819)
XLA Ops:
  7.2 3.3 convert_element_type.66
  10.5 41.3 %reshape.361 = bf16[1,1,1771776]{2,1,0:T(2,128)(2,1)} reshape(bf16[1771776]{0:T(1024)(128)(2,1)S(1)} %convert_element_type.66) | data formatting | bytes 7087104
  57.7 1.2 broadcast_compare_fusion
  58.9 472.0 %all-gather.3.cloned.1.call-done = bf16[4,1,1771776]{2,1,0:T(2,128)(2,1)} async-done(((bf16[1,1,1771776]{2,1,0:T(2,128)(2,1)}), bf16[4,1,1771776]{2,1,0:T(2,128)(2,1)}) %all-gather.3.cloned.1.call-update) | async-done | bytes 14174224 | tf_op jit(solution)/shard_map/all_gather | solution.py:105
  530.9 90.4 %reduce.7 = bf16[4,1771776]{1,0:T(4,128)(2,1)} reduce(bf16[4,1,1771776]{2,1,0:T(2,128)(2,1)} %all-gather.3.cloned.1.call-done, bf16[]{:T(256)} %constant.175), dimensions={1}, to_apply=%all-gather.reduce_sub_computation | reduce | bytes 28348418 | tf_op jit(solution)/shard_map/all_gather | solution.py:105
  621.4 39.5 %reshape.362 = bf16[7087104]{0:T(1024)(128)(2,1)} reshape(bf16[4,1771776]{1,0:T(4,128)(2,1)} %reduce.7) | data formatting | bytes 28348416
  662.2 1.4 slice-done
  663.6 5.2 slice.179
  668.8 4.5 fusion.54
  675.8 2.3 collective-permute-start.1
  678.1 3.0 collective-permute-start
  681.1 3.9 fusion.60
  684.9 1.5 copy.24
  686.5 1.9 slice.189
  688.3 8.2 slice.194
  696.5 9.3 slice.197
  706.6 2.7 maximum_maximum_fusion
  709.3 1.3 fusion.61
  710.6 1.6 copy.23
  712.3 1.7 copy.25
  714.0 10.3 select_reduce_fusion
  724.3 11.6 exponential_reduce_fusion
  735.9 10.9 fusion.36
  748.3 7.4 multiply_convert_fusion.1
  755.8 7.2 fusion.66
  763.0 3.1 multiply_reduce_fusion
  768.2 1.7 convolution_convert_fusion
  769.9 1.4 copy.26
  771.6 12.8 fusion.30
  784.4 16.8 %multiply_convert_fusion = bf16[12,512,1024]{2,1,0:T(8,128)(2,1)} fusion(f32[12,512,1024]{2,1,0:T(8,128)} %get-tuple-element.75, f32[12,512]{1,0:T(8,128)S(1)} %bitcast.68, f32[12,512]{1,0:T(8,128)S(1)} %log_add_fusion, pred[512,1024]{1,0:T(8,128)(4,1)S(1)} %copy-done.11, bf16[512,12,64]{0,2,1:T(8,128)(2,1)S(1)} %bitcast.58, bf16[1024,12,64]{0,2,1:T(8,128)(2,1)} %bitcast.66), kind=kOutput, calls=%fused_computation | convolution fusion | flops 836763648 | bytes 40681472 | tf_op jit(solution)/shard_map/qhd,khd->hqk/dot_general | solution.py:223
  801.2 8.5 fusion.67
  809.7 2.4 copy.27
  812.1 3.5 copy.28
  815.7 2.4 fusion.39
  818.0 1.9 collective-permute-start.2
  820.0 9.4 fusion.62
  829.4 2.3 copy.29
  831.6 3.8 fusion.43
  835.5 3.2 reshape.356
  838.7 11.4 collective-permute-done.2
  850.1 3.5 pad_maximum_fusion.3
  853.5 4.4 collective-permute-start.3
  858.0 2.9 convolution_bitcast_fusion
  860.9 5.9 copy.30
  866.8 5.6 fusion.56
  872.4 10.7 reshape.358
  883.3 3.5 fusion.7
  886.7 4.4 scatter-add.4
  891.2 3.0 dynamic-slice_add_fusion
  894.2 3.3 dynamic_update_slice.3
  899.8 4.7 fusion.21
  904.4 5.2 fusion.34
  909.8 7.9 reshape.355
  917.7 5.2 constant_dynamic-update-slice_fusion.5
  923.1 1.6 constant_dynamic-update-slice_fusion.4
  924.7 9.7 constant_dynamic-update-slice_fusion.3
  934.4 3.8 constant_dynamic-update-slice_fusion.2
  939.4 1.4 copy-done.16
  940.8 7.5 add_select_fusion
  948.3 1.7 fusion.20
  950.1 420.5 %all-reduce.2.cloned.1.call-done = f32[7087104]{0:T(1024)} async-done(((f32[7087104]{0:T(1024)}), f32[7087104]{0:T(1024)}) %all-reduce.2.cloned.1.call-update) | async-done | bytes 28348432 | tf_op jit(solution)/shard_map/psum | solution.py:284
  1370.6 1.5 dynamic_slice.17
  1372.0 5.1 reshape.360
  1377.1 16.8 %multiply_subtract_fusion = (f32[1771776]{0:T(1024)}, f32[1771776]{0:T(1024)}, f32[1771776]{0:T(1024)}) fusion(f32[1771776]{0:T(1024)} %param.15, s32[]{:T(128)S(6)} %mul.237, f32[7087104]{0:T(1024)} %all-reduce.2.cloned.1.call-done, s32[]{:T(128)S(6)} %select_n.67, f32[1771776]{0:T(1024)} %param.16, f32[1771776]{0:T(1024)} %param.17), kind=kLoop, calls=%fused_computation.14 | loop fusion | flops 31891968 | bytes 49609736 | tf_op jit(solution)/shard_map/sub | solution.py:296
  (150 shorter events, 15.8 us)
Async XLA Ops:
  7.2 523.7 %all-gather.3.cloned.1.call-start = ((), (), s32[]{:S(2)}) async-start(), calls=%async_computation.1 | async-start | bytes 35435520 | tf_op jit(solution)/shard_map/all_gather | solution.py:105
  51.8 0.7 copy-start.35
  51.8 5.4 copy-start.6
  51.8 1318.7 %all-reduce.2.cloned.1.call-start = ((), (), s32[]{:S(2)}) async-start(), calls=%async_computation | async-start | bytes 56696832 | tf_op jit(solution)/shard_map/psum | solution.py:284
  55.7 1.4 copy-start.30
  661.6 2.0 slice-start
  668.8 4.6 copy-start.27
  668.8 4.7 copy-start.28
  668.8 12.3 copy-start
  673.4 2.3 copy-start.12
  675.8 30.8 %collective-permute-start.1 = (bf16[196,1536]{1,0:T(8,128)(2,1)}, bf16[196,1536]{1,0:T(8,128)(2,1)}, u32[]{:S(2)}, u32[]{:S(2)}) collective-permute-start(bf16[196,1536]{1,0:T(8,128)(2,1)} %get-tuple-element.62), channel_id=1, source_target_pairs={{1,0},{2,1},{3,2},{4,3},{5,4},{6,5},{7,6},{8,7},{9,8},{10,9},{11,1... | collective-permute-start | bytes 1806344 | tf_op jit(solution)/shard_map/ppermute | solution.py:37
  678.1 28.5 %collective-permute-start = (bf16[196,1536]{1,0:T(8,128)(2,1)}, bf16[196,1536]{1,0:T(8,128)(2,1)}, u32[]{:S(2)}, u32[]{:S(2)}) collective-permute-start(bf16[196,1536]{1,0:T(8,128)(2,1)} %get-tuple-element.61), channel_id=1, source_target_pairs={{0,1},{1,2},{2,3},{3,4},{4,5},{5,6},{6,7},{7,8},{8,9},{9,10},{10,1... | collective-permute-start | bytes 1806344 | tf_op jit(solution)/shard_map/ppermute | solution.py:35
  684.9 1.5 slice-start.1
  696.5 10.0 copy-start.13
  696.5 10.0 copy-start.29
  710.6 3.3 copy-start.11
  714.0 10.3 copy-start.4
  724.3 11.6 copy-start.20
  735.9 11.0 copy-start.7
  735.9 11.0 copy-start.22
  735.9 11.0 copy-start.34
  746.9 24.4 %copy-start.19 = (bf16[12,64,512]{2,1,0:T(8,128)(2,1)}, bf16[12,64,512]{2,1,0:T(8,128)(2,1)S(1)}, u32[]{:S(2)}) copy-start(bf16[12,64,512]{2,1,0:T(8,128)(2,1)S(1)} %fusion.36) | copy-start | bytes 2359300
  746.9 1.3 copy-start.26
  747.0 1.3 copy-start.33
  747.9 18.2 %copy-start.14 = (f32[512,768]{1,0:T(8,128)}, f32[512,768]{1,0:T(8,128)S(1)}, u32[]{:S(2)}) copy-start(f32[512,768]{1,0:T(8,128)S(1)} %get-tuple-element.77) | copy-start | bytes 4718596
  747.9 7.8 slice-start.5
  748.3 7.4 slice-start.6
  748.3 7.4 copy-start.24
  748.3 7.4 copy-start.31
  748.3 14.7 %slice-start.7 = ((s8[4718592]{0:T(1024)(128)(4,1)}), s8[4194304]{0:T(1024)(128)(4,1)S(1)}, s32[]{:S(2)}) async-start(s8[4718592]{0:T(1024)(128)(4,1)} %bitcast.61), calls=%async_computation.9 | async-start | bytes 8388608
  755.7 7.2 slice-start.8
  763.0 3.1 copy-start.37
  766.1 2.1 copy-start.23
  767.1 1.1 copy-start.2
  815.7 4.3 copy-start.5
  818.0 32.0 %collective-permute-start.2 = (f32[196,1536]{1,0:T(8,128)}, f32[196,1536]{1,0:T(8,128)}, u32[]{:S(2)}, u32[]{:S(2)}) collective-permute-start(f32[196,1536]{1,0:T(8,128)} %fusion.39), channel_id=1, source_target_pairs={{0,1},{1,2},{2,3},{3,4},{4,5},{5,6},{6,7},{7,8},{8,9},{9,10},{10,1... | collective-permute-start | bytes 3612680 | tf_op jit(solution)/shard_map/ppermute | solution.py:35
  838.7 19.2 %copy-start.15 = (f32[512,768]{1,0:T(8,128)S(1)}, f32[512,768]{1,0:T(8,128)}, u32[]{:S(2)}) copy-start(f32[512,768]{1,0:T(8,128)} %copy-done.14) | copy-start | bytes 4718596
  838.7 19.2 %copy-start.38 = (bf16[512,3072]{1,0:T(8,128)(2,1)S(1)}, bf16[512,3072]{1,0:T(8,128)(2,1)}, u32[]{:S(2)}) copy-start(bf16[512,3072]{1,0:T(8,128)(2,1)} %copy-done.37) | copy-start | bytes 9437188
  853.5 37.6 %collective-permute-start.3 = (f32[196,1536]{1,0:T(8,128)}, f32[196,1536]{1,0:T(8,128)}, u32[]{:S(2)}, u32[]{:S(2)}) collective-permute-start(f32[196,1536]{1,0:T(8,128)} %get-tuple-element.53), channel_id=1, source_target_pairs={{1,0},{2,1},{3,2},{4,3},{5,4},{6,5},{7,6},{8,7},{9,8},{10,9},{11,1... | collective-permute-start | bytes 3612680 | tf_op jit(solution)/shard_map/ppermute | solution.py:37
  860.9 5.9 copy-start.25
  860.9 5.9 copy-start.36
  891.2 3.0 copy-start.1
  897.5 1.1 copy-start.8
  897.5 2.2 copy-start.17
  899.8 4.7 copy-start.18
  917.7 5.3 copy-start.10
  923.1 11.3 slice-start.2
  924.7 9.7 slice-start.3
  924.7 9.7 slice-start.4
  939.4 1.4 copy-start.16
  939.4 1.4 copy-start.32
  940.8 7.5 copy-start.3
  940.8 7.5 copy-start.9
  940.8 7.5 copy-start.21
Sparse Core Ops, SparseCore 0:
  51.9 478.9 all-gather.2
  939.5 430.9 all-reduce.1
where the time goes:
time: 1410 us; the launch traced here: 1400 us
  waiting for transfers between devices  904 us (64%)
  local copies, waits for them, and re-layouts  197 us (14%)
  other arithmetic  148 us (10%)
  matrix products  123 us (9%)
  between operations  17 us (1%)
    all_gather x1, waiting for transfers between devices, shards(): lax.all_gather(params.astype(jnp.bfloat16), 'shard', axis=0, tiled=True)  472 us
    psum x1, waiting for transfers between devices, shards(): summed = lax.psum(grad_flat, ('dp', 'shard'))  420 us
    unnamed x100, local copies, waits for them, and re-layouts  113 us
    all_gather x1, other arithmetic, shards(): lax.all_gather(params.astype(jnp.bfloat16), 'shard', axis=0, tiled=True)  90.4 us
    slice x9, local copies, waits for them, and re-layouts, unpack(): pieces.append(flat_vec[cursor:cursor + extent])  29.8 us
  transfers between devices with their start and end apart: 6, of which 3 were waited for; matrix products, arithmetic and copies ran while one was open for 6% of the time, Pallas kernels for 0%

commit v1 on v0

--- a/solution.py
+++ b/solution.py
@@ -1,6 +1,10 @@
+import functools
+
 import jax
 import jax.numpy as jnp
 from jax import lax
+from jax.experimental import pallas as pl
+from jax.experimental.pallas import tpu as pltpu
 from jax.sharding import PartitionSpec as P
 
 D = 768
@@ -22,6 +26,521 @@
 adam_eps = 1e-08
 sqrt_half = 0.7071067811865476
 inv_root_two_pi = 0.3989422804014327
+
+
+MESH = pl.DeviceIdType.MESH
+LANES = 128
+MARGIN = 64
+
+
+def geometry(n_dp, n_shard):
+    total = 4 * D * D + 2 * D * FF + 8 * D + FF
+    shard_lines = total // n_shard // LANES
+    piece = -(-shard_lines // n_dp // 32) * 32
+    piece = -(-(-(-shard_lines // n_dp)) // 32) * 32
+    return shard_lines, piece, piece * n_dp
+
+
+def bit_list(n_dp):
+    count = n_dp.bit_length() - 1
+    return count, [list(range(1, count)), list(range(count - 1, 0, -1))]
+
+
+def bits_of(index, count):
+    return [lax.rem(lax.div(index, 1 << b), 2) for b in range(count)]
+
+
+def flipped(index, bits, which):
+    return index + sum((1 << b) * (1 - 2 * bits[b]) for b in which)
+
+
+def greet(n_dp, n_shard, place, level, bits):
+    barrier = pltpu.get_barrier_semaphore()
+    peers = [(place, lax.rem(level + j, n_shard)) for j in range(1, n_shard)]
+    peers += [(flipped(place, bits, [b]), level) for b in range(len(bits))]
+    for peer in peers:
+        pl.semaphore_signal(barrier, inc=1, device_id=peer, device_id_type=MESH)
+    pl.semaphore_wait(barrier, len(peers))
+
+
+def subsets(order):
+    found = [[]]
+    for b in order:
+        found = found + [kept + [b] for kept in found]
+    return found
+
+
+def gather_kernel(n_dp, n_shard, half, own, out, z_send, z_recv, d_send, d_recv):
+    place = lax.axis_index("dp")
+    level = lax.axis_index("shard")
+    count, orders = bit_list(n_dp)
+    bits = bits_of(place, count)
+    greet(n_dp, n_shard, place, level, bits)
+    started = []
+
+    def push(src, dst, send, recv, target):
+        copy = pltpu.make_async_remote_copy(
+            src_ref=src,
+            dst_ref=dst,
+            send_sem=send,
+            recv_sem=recv,
+            device_id=target,
+            device_id_type=MESH,
+        )
+        copy.start()
+        started.append(copy)
+
+    for side in range(2):
+        for j in range(1, n_shard):
+            push(
+                own.at[place, side],
+                out.at[level, place, side],
+                z_send.at[j - 1, side],
+                z_recv.at[j - 1, side],
+                (place, lax.rem(level + j, n_shard)),
+            )
+    chunks = [(j, side) for j in range(1, n_shard) for side in range(2)]
+
+    def advance(chunk, stage):
+        j, side = chunks[chunk]
+        source = lax.rem(level - j + n_shard, n_shard)
+        order = orders[side] + [0]
+
+        def arrived(piece, sem):
+            pltpu.make_async_remote_copy(
+                src_ref=own.at[place, side],
+                dst_ref=out.at[source, piece, side],
+                send_sem=z_send.at[0, 0],
+                recv_sem=sem,
+                device_id=(place, level),
+                device_id_type=MESH,
+            ).wait_recv()
+
+        if stage == 0:
+            arrived(place, z_recv.at[j - 1, side])
+        else:
+            partner = flipped(place, bits, [order[stage - 1]])
+            for slot, which in enumerate(subsets(order[: stage - 1])):
+                arrived(
+                    flipped(place, bits, which + [order[stage - 1]]),
+                    d_recv.at[chunk, (1 << (stage - 1)) - 1 + slot],
+                )
+        if stage < count:
+            partner = flipped(place, bits, [order[stage]])
+            for slot, which in enumerate(subsets(order[:stage])):
+                piece = flipped(place, bits, which)
+                index = (1 << stage) - 1 + slot
+                push(
+                    out.at[source, piece, side],
+                    out.at[source, piece, side],
+                    d_send.at[chunk, index],
+                    d_recv.at[chunk, index],
+                    (partner, level),
+                )
+
+    for tick in range(len(chunks) + count):
+        for stage in range(count + 1):
+            chunk = tick - stage
+            if 0 <= chunk < len(chunks):
+                advance(chunk, stage)
+    for copy in started:
+        copy.wait_send()
+
+
+def gather_weights(n_dp, n_shard, own):
+    shard_lines, piece, padded = geometry(n_dp, n_shard)
+    half = piece // 2
+    chunks = 2 * (n_shard - 1)
+    return pl.pallas_call(
+        functools.partial(gather_kernel, n_dp, n_shard, half),
+        out_shape=jax.ShapeDtypeStruct((n_shard, n_dp, 2, half, LANES), jnp.bfloat16),
+        in_specs=[pl.BlockSpec(memory_space=pltpu.HBM)],
+        out_specs=pl.BlockSpec(memory_space=pltpu.HBM),
+        scratch_shapes=[
+            pltpu.SemaphoreType.DMA((n_shard - 1, 2)),
+            pltpu.SemaphoreType.DMA((n_shard - 1, 2)),
+            pltpu.SemaphoreType.DMA((chunks, n_dp - 1)),
+            pltpu.SemaphoreType.DMA((chunks, n_dp - 1)),
+        ],
+        compiler_params=pltpu.CompilerParams(collective_id=1, has_side_effects=True),
+        name="gather_weights",
+    )(own)
+
+
+def weight_plan(n_shard, shard_lines):
+    sizes = [(D, 3 * D), (D, D), (D, FF), (FF, D)]
+    plan = [[] for _ in range(n_shard)]
+    cursor = 0
+    for which, (rows, columns) in enumerate(sizes):
+        width = columns // LANES
+        first = 0
+        for s in range(n_shard):
+            stop = (s + 1) * shard_lines
+            last = min(rows, max(first, (stop - cursor) // width))
+            last = last if last == rows else last // 128 * 128
+            if last > first:
+                plan[s].append((which, first, last, width, cursor + first * width - s * shard_lines))
+                first = last
+        cursor += rows * width
+    return plan, cursor
+
+
+def layout_kernel(n_shard, shard_lines, padded, own, got, wqkv, wout, win, wback, vec, raw, wide, sem):
+    level = lax.axis_index("shard")
+    plan, tail = weight_plan(n_shard, shard_lines)
+    targets = [wqkv, wout, win, wback]
+
+    def load(s, slot):
+        @pl.when(level == s)
+        def _():
+            pltpu.make_async_copy(own, raw.at[slot], sem.at[slot]).start()
+
+        @pl.when(level != s)
+        def _():
+            pltpu.make_async_copy(got.at[s], raw.at[slot], sem.at[slot]).start()
+
+    load(0, 0)
+    for s in range(n_shard):
+        slot = s % 2
+        pltpu.make_async_copy(own, raw.at[slot], sem.at[slot]).wait()
+        if s + 1 < n_shard:
+            load(s + 1, 1 - slot)
+        if s:
+            wide[0:MARGIN, :] = wide[shard_lines : shard_lines + MARGIN, :]
+
+        def spread(i, carry):
+            at = pl.multiple_of(i * 128, 128)
+            wide[pl.ds(MARGIN + at, 128), :] = raw[slot, pl.ds(at, 128), :].astype(jnp.float32)
+            return carry
+
+        lax.fori_loop(0, padded // 128, spread, 0)
+        for which, first, last, width, offset in plan[s]:
+            target = targets[which]
+
+            def rows(i, carry):
+                at = pl.multiple_of(first + i * 16, 16)
+                line = MARGIN + offset + i * (16 * width)
+                for c in range(width):
+                    target[pl.ds(at, 16), c * LANES : (c + 1) * LANES] = wide[
+                        pl.ds(line + c, 16, stride=width), :
+                    ].astype(jnp.bfloat16)
+                return carry
+
+            lax.fori_loop(0, (last - first) // 16, rows, 0)
+    start = MARGIN + tail - (n_shard - 1) * shard_lines
+    vec[...] = wide[start : start + vec.shape[0], :]
+
+
+def lay_out_weights(n_dp, n_shard, own, got):
+    shard_lines, piece, padded = geometry(n_dp, n_shard)
+    count = (8 * D + FF) // LANES
+    shapes = [(D, 3 * D), (D, D), (D, FF), (FF, D)]
+    return pl.pallas_call(
+        functools.partial(layout_kernel, n_shard, shard_lines, padded),
+        out_shape=[jax.ShapeDtypeStruct(shape, jnp.bfloat16) for shape in shapes]
+        + [jax.ShapeDtypeStruct((count, LANES), jnp.float32)],
+        in_specs=[pl.BlockSpec(memory_space=pltpu.HBM)] * 2,
+        out_specs=[pl.BlockSpec(memory_space=pltpu.VMEM)] * 5,
+        scratch_shapes=[
+            pltpu.VMEM((2, padded, LANES), jnp.bfloat16),
+            pltpu.VMEM((MARGIN + padded, LANES), jnp.float32),
+            pltpu.SemaphoreType.DMA((2,)),
+        ],
+        compiler_params=pltpu.CompilerParams(vmem_limit_bytes=60 << 20),
+        name="lay_out_weights",
+    )(own.reshape(padded, LANES), got.reshape(n_shard, padded, LANES))
+
+
+def weight_grad_kernel(
+    n_shard, shard_lines, padded, feed_one, joined, attended, middle, feed_two, slope, activated, tangent, vec, out, wide, narrow, sem
+):
+    lefts = [feed_one, attended, feed_two, activated]
+    rights = [joined, middle, slope, tangent]
+    sizes = [(D, 3 * D), (D, D), (D, FF), (FF, D)]
+    cursor = 0
+    plan = [[] for _ in range(n_shard)]
+    for which, (rows, columns) in enumerate(sizes):
+        width = columns // LANES
+        for s in range(n_shard):
+            begin, stop = s * shard_lines, (s + 1) * shard_lines
+            first = max(0, (begin - cursor) // width)
+            last = min(rows, -(-(stop - cursor) // width))
+            if last > first:
+                first = first // 128 * 128
+                plan[s].append((which, first, last, width, cursor - begin))
+        cursor += rows * width
+    tail = cursor - (n_shard - 1) * shard_lines
+
+    def product(which, row, width, group):
+        return lax.dot_general(
+            lefts[which][:, pl.ds(row, 128)],
+            rights[which][:, group * 768 : (group + 1) * 768],
+            (((0,), (0,)), ((), ())),
+            preferred_element_type=jnp.float32,
+        )
+
+    for s in range(n_shard):
+        for which, first, last, width, offset in plan[s]:
+            full = (last - first) // 128
+
+            def block(i, carry):
+                row = pl.multiple_of(first + i * 128, 128)
+                line = MARGIN + offset + row * width
+                for group in range(width // 6):
+                    tile = product(which, row, width, group)
+                    for c in range(6):
+                        wide[pl.ds(line + group * 6 + c, 128, stride=width), :] = tile[
+                            :, c * LANES : (c + 1) * LANES
+                        ]
+                return carry
+
+            if full:
+                lax.fori_loop(0, full, block, 0)
+            row = first + full * 128
+            rest = -(-(last - row) // 8) * 8
+            if rest:
+                line = MARGIN + offset + row * width
+                for group in range(width // 6):
+                    tile = product(which, row, width, group)
+                    for c in range(6):
+                        wide[pl.ds(line + group * 6 + c, rest, stride=width), :] = tile[
+                            :rest, c * LANES : (c + 1) * LANES
+                        ]
+        if s == n_shard - 1:
+            wide[MARGIN + tail : MARGIN + tail + vec.shape[0], :] = vec[...]
+        slot = s % 2
+        if s >= 2:
+            pltpu.make_async_copy(narrow.at[slot], out.at[s - 2], sem.at[slot]).wait()
+
+        def pack(i, carry):
+            at = pl.multiple_of(i * 128, 128)
+            narrow[slot, pl.ds(at, 128), :] = wide[pl.ds(MARGIN + at, 128), :].astype(jnp.bfloat16)
+            return carry
+
+        lax.fori_loop(0, padded // 128, pack, 0)
+        pltpu.make_async_copy(narrow.at[slot], out.at[s], sem.at[slot]).start()
+    for s in range(n_shard - 2, n_shard):
+        pltpu.make_async_copy(narrow.at[s % 2], out.at[s], sem.at[s % 2]).wait()
+
+
+def weight_grads(n_dp, n_shard, *operands):
+    shard_lines, piece, padded = geometry(n_dp, n_shard)
+    return pl.pallas_call(
+        functools.partial(weight_grad_kernel, n_shard, shard_lines, padded),
+        out_shape=jax.ShapeDtypeStruct((n_shard, padded, LANES), jnp.bfloat16),
+        in_specs=[pl.BlockSpec(memory_space=pltpu.VMEM)] * 9,
+        out_specs=pl.BlockSpec(memory_space=pltpu.HBM),
+        scratch_shapes=[
+            pltpu.VMEM((MARGIN + padded + 128, LANES), jnp.float32),
+            pltpu.VMEM((2, padded, LANES), jnp.bfloat16),
+            pltpu.SemaphoreType.DMA((2,)),
+        ],
+        compiler_params=pltpu.CompilerParams(vmem_limit_bytes=60 << 20),
+        name="weight_grads",
+    )(*operands)
+
+
+def reduce_kernel(n_dp, n_shard, half, grads, out, *scratch):
+    count, orders = bit_list(n_dp)
+    acc, got_core = scratch[0], scratch[1]
+    got_bits = scratch[2 : 1 + count]
+    got_z, final = scratch[1 + count : 3 + count]
+    load_sem, core_send, core_recv, bit_send, bit_recv, z_send, z_recv, g_send, g_recv, keep_sem = scratch[
+        3 + count :
+    ]
+    place = lax.axis_index("dp")
+    level = lax.axis_index("shard")
+    bits = bits_of(place, count)
+    pairs = n_dp // 2
+    chunks = [(j, side) for j in list(range(1, n_shard)) + [0] for side in range(2)]
+    step = 176 if half % 176 == 0 else 32
+    greet(n_dp, n_shard, place, level, bits)
+    started = []
+
+    def push(src, dst, send, recv, target):
+        copy = pltpu.make_async_remote_copy(
+            src_ref=src,
+            dst_ref=dst,
+            send_sem=send,
+            recv_sem=recv,
+            device_id=target,
+            device_id_type=MESH,
+        )
+        copy.start()
+        started.append(copy)
+
+    def landed(buffer, sem):
+        pltpu.make_async_remote_copy(
+            src_ref=buffer,
+            dst_ref=buffer,
+            send_sem=z_send.at[0, 0],
+            recv_sem=sem,
+            device_id=(place, level),
+            device_id_type=MESH,
+        ).wait_recv()
+
+    core = bits[0]
+    partner = flipped(place, bits, [0])
+    for chunk, (j, side) in enumerate(chunks):
+        target = lax.rem(level + j, n_shard)
+        for m in range(pairs):
+            push(
+                grads.at[target, 2 * m + 1 - core, side],
+                got_core.at[chunk, m],
+                core_send.at[chunk, m],
+                core_recv.at[chunk, m],
+                (partner, level),
+            )
+            pltpu.make_async_copy(
+                grads.at[target, 2 * m + core, side], acc.at[chunk, m], load_sem.at[chunk, m]
+            ).start()
+
+    def add(into, other):
+        def body(i, carry):
+            at = pl.multiple_of(i * step, 16)
+            total = into[pl.ds(at, step), :].astype(jnp.float32) + other[pl.ds(at, step), :].astype(
+                jnp.float32
+            )
+            into[pl.ds(at, step), :] = total.astype(jnp.bfloat16)
+            return carry
+
+        lax.fori_loop(0, half // step, body, 0)
+
+    def members(order, stage, flip):
+        fixed = order[:stage]
+        base = sum((bits[b] if b != flip else 1 - bits[b]) * (1 << (b - 1)) for b in fixed)
+        return [base + sum(1 << (b - 1) for b in which) for which in subsets(order[stage:])]
+
+    def advance(chunk, stage):
+        j, side = chunks[chunk]
+        order = orders[side]
+        if stage == 0:
+            for m in range(pairs):
+                pltpu.make_async_copy(
+                    grads.at[0, 2 * m + core, side], acc.at[chunk, m], load_sem.at[chunk, m]
+                ).wait()
+                landed(got_core.at[chunk, m], core_recv.at[chunk, m])
+                add(acc.at[chunk, m], got_core.at[chunk, m])
+        else:
+            for slot, m in enumerate(members(order, stage, None)):
+                buffer = got_bits[stage - 1].at[chunk, slot]
+                landed(buffer, bit_recv.at[stage - 1, chunk, slot])
+                add(acc.at[chunk, m], buffer)
+        if stage < count - 1:
+            flip = order[stage]
+            target = flipped(place, bits, [flip])
+            for slot, m in enumerate(members(order, stage + 1, flip)):
+                push(
+                    acc.at[chunk, m],
+                    got_bits[stage].at[chunk, slot],
+                    bit_send.at[stage, chunk, slot],
+                    bit_recv.at[stage, chunk, slot],
+                    (target, level),
+                )
+        elif j:
+            (m,) = members(order, stage, None)
+            push(
+                acc.at[chunk, m],
+                got_z.at[j - 1, side],
+                z_send.at[j - 1, side],
+                z_recv.at[j - 1, side],
+                (place, lax.rem(level + j, n_shard)),
+            )
+
+    for tick in range(len(chunks) + count - 1):
+        for stage in range(count):
+            chunk = tick - stage
+            if 0 <= chunk < len(chunks):
+                advance(chunk, stage)
+
+    mine = sum(bits[b] * (1 << (b - 1)) for b in range(1, count))
+    keeps = []
+    for side in range(2):
+        chunk = chunks.index((0, side))
+        for j in range(1, n_shard):
+            landed(got_z.at[j - 1, side], z_recv.at[j - 1, side])
+
+        def body(i, carry):
+            at = pl.multiple_of(i * step, 16)
+            total = acc[chunk, mine, pl.ds(at, step), :].astype(jnp.float32)
+            for j in range(1, n_shard):
+                total = total + got_z[j - 1, side, pl.ds(at, step), :].astype(jnp.float32)
+            final[side, pl.ds(at, step), :] = total.astype(jnp.bfloat16)
+            return carry
+
+        lax.fori_loop(0, half // step, body, 0)
+        keep = pltpu.make_async_copy(final.at[side], out.at[place, side], keep_sem.at[side])
+        keep.start()
+        keeps.append(keep)
+        push(
+            final.at[side],
+            out.at[place, side],
+            g_send.at[side, 0],
+            g_recv.at[side, 0],
+            (flipped(place, bits, [orders[side][0]]), level),
+        )
+    for stage in range(1, count + 1):
+        for side in range(2):
+            order = orders[side] + [0]
+            for slot, which in enumerate(subsets(order[: stage - 1])):
+                landed(
+                    out.at[flipped(place, bits, which + [order[stage - 1]]), side],
+                    g_recv.at[side, (1 << (stage - 1)) - 1 + slot],
+                )
+            if stage < count:
+                target = flipped(place, bits, [order[stage]])
+                for slot, which in enumerate(subsets(order[:stage])):
+                    piece = flipped(place, bits, which)
+                    index = (1 << stage) - 1 + slot
+                    push(
+                        final.at[side] if not which else out.at[piece, side],
+                        out.at[piece, side],
+                        g_send.at[side, index],
+                        g_recv.at[side, index],
+                        (target, level),
+                    )
+    for keep in keeps:
+        keep.wait()
+    for copy in started:
+        copy.wait_send()
+
+
+def reduce_grads(n_dp, n_shard, grads):
+    shard_lines, piece, padded = geometry(n_dp, n_shard)
+    half = piece // 2
+    count = n_dp.bit_length() - 1
+    chunks = 2 * n_shard
+    pairs = n_dp // 2
+    got_bits = [
+        pltpu.VMEM((chunks, pairs >> t, half, LANES), jnp.bfloat16) for t in range(1, count)
+    ]
+    return pl.pallas_call(
+        functools.partial(reduce_kernel, n_dp, n_shard, half),
+        out_shape=jax.ShapeDtypeStruct((n_dp, 2, half, LANES), jnp.bfloat16),
+        in_specs=[pl.BlockSpec(memory_space=pltpu.HBM)],
+        out_specs=pl.BlockSpec(memory_space=pltpu.HBM),
+        scratch_shapes=[
+            pltpu.VMEM((chunks, pairs, half, LANES), jnp.bfloat16),
+            pltpu.VMEM((chunks, pairs, half, LANES), jnp.bfloat16),
+            *got_bits,
+            pltpu.VMEM((n_shard - 1, 2, half, LANES), jnp.bfloat16),
+            pltpu.VMEM((2, half, LANES), jnp.bfloat16),
+            pltpu.SemaphoreType.DMA((chunks, pairs)),
+            pltpu.SemaphoreType.DMA((chunks, pairs)),
+            pltpu.SemaphoreType.DMA((chunks, pairs)),
+            pltpu.SemaphoreType.DMA((count - 1, chunks, pairs // 2)),
+            pltpu.SemaphoreType.DMA((count - 1, chunks, pairs // 2)),
+            pltpu.SemaphoreType.DMA((n_shard - 1, 2)),
+            pltpu.SemaphoreType.DMA((n_shard - 1, 2)),
+            pltpu.SemaphoreType.DMA((2, n_dp - 1)),
+            pltpu.SemaphoreType.DMA((2, n_dp - 1)),
+            pltpu.SemaphoreType.DMA((2,)),
+        ],
+        compiler_params=pltpu.CompilerParams(
+            collective_id=2, has_side_effects=True, vmem_limit_bytes=60 << 20
+        ),
+        name="reduce_grads",
+    )(grads.reshape(n_shard, n_dp, 2, half, LANES))
 
 
 def extended_2(cells, sides, width):
@@ -68,23 +587,6 @@
     return inverse * (scaled - first_mean - normed * second)
 
 
-def unpack(flat_vec):
-    lengths = [3 * D * D, D * D, D * FF, FF * D, 8 * D, FF]
-    pieces = []
-    cursor = 0
-    for extent in lengths:
-        pieces.append(flat_vec[cursor : cursor + extent])
-        cursor = cursor + extent
-    return (
-        pieces[0].reshape(D, 3 * D),
-        pieces[1].reshape(D, D),
-        pieces[2].reshape(D, FF),
-        pieces[3].reshape(FF, D),
-        pieces[4].reshape(8, D),
-        pieces[5],
-    )
-
-
 def split_heads(matrix):
     return matrix.reshape(matrix.shape[0], HEADS, HD)
 
@@ -102,10 +604,17 @@
 def shards(block_input, cotangent, token_bounds, params, first_moment, second_moment):
     rows_here = block_input.shape[0]
     own_len = params.shape[0]
-    gathered = lax.all_gather(params.astype(jnp.bfloat16), "shard", axis=0, tiled=True)
-    weight_qkv, weight_out, weight_in, weight_back, vectors, bias_raw = unpack(gathered)
-    vector_f = vectors.astype(jnp.float32)
-    bias_in = bias_raw.astype(jnp.float32)
+    n_dp, n_shard = lax.axis_size("dp"), lax.axis_size("shard")
+    shard_lines, piece, padded = geometry(n_dp, n_shard)
+    own_weights = jnp.pad(params.astype(jnp.bfloat16), (0, padded * LANES - own_len)).reshape(
+        n_dp, 2, piece // 2, LANES
+    )
+    gathered = gather_weights(n_dp, n_shard, own_weights)
+    weight_qkv, weight_out, weight_in, weight_back, lines = lay_out_weights(
+        n_dp, n_shard, own_weights, gathered
+    )
+    vector_f = lines[: 8 * D // LANES].reshape(8, D)
+    bias_in = lines[8 * D // LANES :].reshape(FF)
     gain_one, shift_one, bias_q, bias_v = (vector_f[0], vector_f[1], vector_f[2], vector_f[3])
     bias_out, gain_two, shift_two, bias_back = (vector_f[4], vector_f[5], vector_f[6], vector_f[7])
     start_tok = token_bounds[0, 0]
@@ -190,22 +699,17 @@
     activations = jnp.where(is_live[:, None], result, 0.0)
     tangent_b = jnp.where(is_live[:, None], cotangent, jnp.zeros_like(cotangent))
     tangent = tangent_b.astype(jnp.float32)
-    grad_back = jnp.einsum("tf,td->fd", activated, tangent_b, preferred_element_type=jnp.float32)
     grad_bias_back = jnp.sum(tangent, axis=0)
     slope_in = jnp.einsum(
         "td,fd->tf", tangent_b, weight_back, preferred_element_type=jnp.float32
     ) * gelu_slope(preact)
     grad_bias_in = jnp.sum(slope_in, axis=0)
     slope_feed = slope_in.astype(jnp.bfloat16)
-    grad_in = jnp.einsum("td,tf->df", second_feed, slope_feed, preferred_element_type=jnp.float32)
     back_two = jnp.einsum("tf,df->td", slope_feed, weight_in, preferred_element_type=jnp.float32)
     grad_gain_two = jnp.sum(back_two * second_normed, axis=0)
     grad_shift_two = jnp.sum(back_two, axis=0)
     middle_grad = tangent + norm_backward(back_two, second_normed, second_inv, gain_two)
     middle_feed = middle_grad.astype(jnp.bfloat16)
-    grad_out = jnp.einsum(
-        "td,te->de", attended_list, middle_feed, preferred_element_type=jnp.float32
-    )
     grad_bias_out = jnp.sum(middle_grad, axis=0)
     attended_grad = jnp.einsum(
         "te,de->td", middle_feed, weight_out, preferred_element_type=jnp.float32
@@ -252,7 +756,6 @@
     grad_bias_q = jnp.sum(query_grads, axis=0)
     grad_bias_v = jnp.sum(own_grad[:, D:], axis=0)
     joined = jnp.concatenate([query_grads, own_grad], axis=1).astype(jnp.bfloat16)
-    grad_qkv = jnp.einsum("td,te->de", first_feed, joined, preferred_element_type=jnp.float32)
     back_one = jnp.einsum("te,de->td", joined, weight_qkv, preferred_element_type=jnp.float32)
     grad_gain_one = jnp.sum(back_one * first_normed, axis=0)
     grad_shift_one = jnp.sum(back_one, axis=0)
@@ -270,19 +773,23 @@
             grad_bias_back,
         ]
     )
-    grad_flat = jnp.concatenate(
-        [
-            grad_qkv.reshape(-1),
-            grad_out.reshape(-1),
-            grad_in.reshape(-1),
-            grad_back.reshape(-1),
-            vector_grad.reshape(-1),
-            grad_bias_in,
-        ]
-    )
-    piece_len = own_len // lax.axis_size("dp")
-    summed = lax.psum(grad_flat, ("dp", "shard"))
-    grad_shard = lax.dynamic_slice_in_dim(summed, lax.axis_index("shard") * own_len, own_len, 0)
+    vector_lines = jnp.concatenate([vector_grad.reshape(-1), grad_bias_in]).reshape(-1, LANES)
+    flat_grads = weight_grads(
+        n_dp,
+        n_shard,
+        first_feed,
+        joined,
+        attended_list,
+        middle_feed,
+        second_feed,
+        slope_feed,
+        activated,
+        tangent_b,
+        vector_lines,
+    )
+    reduced = reduce_grads(n_dp, n_shard, flat_grads).reshape(-1)
+    piece_len = own_len // n_dp
+    grad_shard = reduced[:own_len].astype(jnp.float32)
     grad_piece = lax.dynamic_slice_in_dim(
         grad_shard, lax.axis_index("dp") * piece_len, piece_len, 0
     )

time: 1410 us -> 510 us (0.36)
  waiting for transfers between devices: 904 us -> 49.8 us
  Pallas kernels: 0 us -> 224 us
  local copies, waits for them, and re-layouts: 197 us -> 48 us
  other arithmetic: 148 us -> 63.2 us
  matrix products: 123 us -> 97.9 us
    all_gather x1 -> x0, waiting for transfers between devices: 472 us -> none  [shards(): lax.all_gather(params.astype(jnp.bfloat16), 'shard', axis=0, tiled=True)]
    psum x1 -> x0, waiting for transfers between devices: 420 us -> none  [shards(): summed = lax.psum(grad_flat, ('dp', 'shard'))]
    pallas_call x0 -> x4, Pallas kernels: none -> 224 us  [the longest x1 104 us: reduce_grads(): pl.pallas_call(functools.partial(reduce_kernel, n_dp, n_shard, half), out...]
    unnamed x100 -> x64, local copies, waits for them, and re-layouts: 113 us -> 9.08 us
    all_gather x1 -> x0, other arithmetic: 90.4 us -> none  [shards(): lax.all_gather(params.astype(jnp.bfloat16), 'shard', axis=0, tiled=True)]
    slice x10 -> x0, local copies, waits for them, and re-layouts: 30.4 us -> none  [the longest x9 29.8 us: unpack(): pieces.append(flat_vec[cursor:cursor + extent])]
    ppermute x2, waiting for transfers between devices: 11.4 us -> 36.4 us  [extended_2(): lax.ppermute(tail, axis, [(i, (i + 1) % count) for i in range(ends)])]
    reshape x3 -> x0, local copies, waits for them, and re-layouts: 21.9 us -> none  [the longest x1 10.7 us: shards(): grad_back.reshape(-1)]
  transfers between devices with their start and end apart: 6 -> 4, of which waited for: 3 -> 3; matrix products, arithmetic and copies ran while one was open for 6% -> 6% of each run, Pallas kernels for 0% -> 0%
where the time goes in v1:
time: 510 us; the launch traced here: 505 us
  Pallas kernels  224 us (44%)
  matrix products  97.9 us (19%)
  other arithmetic  63.2 us (12%)
  waiting for transfers between devices  49.8 us (10%)
  local copies, waits for them, and re-layouts  48 us (9%)
  starting transfers between devices  18 us (4%)
    pallas_call x1, Pallas kernels, reduce_grads(): pl.pallas_call(functools.partial(reduce_kernel, n_dp, n_shard, half), out...  104 us
    pallas_call x1, Pallas kernels, gather_weights(): pl.pallas_call(functools.partial(gather_kernel, n_dp, n_shard, half), out...  77 us
    ppermute x2, waiting for transfers between devices, extended_2(): lax.ppermute(tail, axis, [(i, (i + 1) % count) for i in range(ends)])  36.4 us
    pallas_call x1, Pallas kernels, weight_grads(): pl.pallas_call(functools.partial(weight_grad_kernel, n_shard, shard_lines...  27.5 us
    dot_general x1, matrix products, shards(): jnp.einsum('qhd,khd->hqk', grad_part, value_part, preferred_element_type=...  16.7 us
    pallas_call x1, Pallas kernels, lay_out_weights(): pl.pallas_call(functools.partial(layout_kernel, n_shard, shard_lines, pad...  16.3 us
    sub x1, other arithmetic, shards(): params - learn_rate * (first_hat / (jnp.sqrt(second_hat) + adam_eps) + de...  14.9 us
    ppermute x2, waiting for transfers between devices, extended_2(): lax.ppermute(head, axis, [((i + 1) % count, i) for i in range(ends)])  13.4 us
  transfers between devices with their start and end apart: 4, of which 3 were waited for; matrix products, arithmetic and copies ran while one was open for 6% of the time, Pallas kernels for 0%

profile of v1, /device:TPU:1, one launch (start us, length us, event | category | flops | bytes accessed | tf_op | source)
XLA Modules:
  0.0 504.7 jit_solution(3034580352638618760)
XLA Ops:
  0.6 1.3 fusion.50
  3.2 1.3 convert_reduce_fusion
  4.6 1.5 fusion.22
  6.1 3.3 convert_element_type.60
  9.4 3.8 fusion.47
  13.2 77.0 %gather_weights.1 = bf16[4,8,2,880,128]{4,3,2,1,0:T(8,128)(2,1)} custom-call(bf16[8,2,880,128]{3,2,1,0:T(8,128)(2,1)} %bitcast.76), custom_call_target="tpu_custom_call" | custom-call | tf_op jit(solution)/shard_map/gather_weights/pallas_call | solution.py:154
  90.3 16.3 %lay_out_weights.1 = (bf16[768,2304]{1,0:T(8,128)(2,1)}, bf16[768,768]{1,0:T(8,128)(2,1)}, bf16[768,3072]{1,0:T(8,128)(2,1)}, bf16[3072,768]{1,0:T(8,128)(2,1)}, f32[72,128]{1,0:T(8,128)}) custom-call(bf16[14080,128]{1,0:T(8,128)(2,1)} %get-tuple-element.70.own, bf16[4,14080,128]{2,1,0:T(8,128)(2,1)} %bitcast.72), custom_call_target="tpu_custom_call" | custom-call | tf_op jit(solution)/shard_map/lay_out_weights/pallas_call | solution.py:238
  106.5 0.8 slice_bitcast_fusion.1
  107.4 1.3 convert_reduce_fusion.1
  108.7 4.3 fusion.52
  113.0 2.2 copy-done.14
  115.3 3.0 fusion.25
  118.3 1.1 fusion.37
  119.4 3.1 collective-permute-start
  122.6 6.1 %collective-permute-start.1 = (bf16[196,1536]{1,0:T(8,128)(2,1)}, bf16[196,1536]{1,0:T(8,128)(2,1)}, u32[]{:S(2)}, u32[]{:S(2)}) collective-permute-start(bf16[196,1536]{1,0:T(8,128)(2,1)} %get-tuple-element.76), channel_id=1, source_target_pairs={{1,0},{2,1},{3,2},{4,3},{5,4},{6,5},{7,6},{8,7},{9,8},{10,9},{11,1... | collective-permute-start | bytes 1806344 | tf_op jit(solution)/shard_map/ppermute | solution.py:556
  130.6 1.4 copy.24
  132.9 1.1 broadcast_compare_fusion
  134.0 7.0 %collective-permute-done = bf16[196,1536]{1,0:T(8,128)(2,1)} collective-permute-done((bf16[196,1536]{1,0:T(8,128)(2,1)}, bf16[196,1536]{1,0:T(8,128)(2,1)}, u32[]{:S(2)}, u32[]{:S(2)}) %collective-permute-start) | collective-permute-done | bytes 602144 | tf_op jit(solution)/shard_map/ppermute | solution.py:554
  141.1 13.4 %collective-permute-done.1 = bf16[196,1536]{1,0:T(8,128)(2,1)} collective-permute-done((bf16[196,1536]{1,0:T(8,128)(2,1)}, bf16[196,1536]{1,0:T(8,128)(2,1)}, u32[]{:S(2)}, u32[]{:S(2)}) %collective-permute-start.1) | collective-permute-done | bytes 602144 | tf_op jit(solution)/shard_map/ppermute | solution.py:556
  154.4 2.7 maximum_maximum_fusion
  157.2 1.9 fusion.48
  159.0 1.7 copy.25
  160.7 3.1 copy.23
  163.9 11.3 %select_reduce_fusion = (f32[12,512]{1,0:T(8,128)S(1)}, f32[12,512,1024]{2,1,0:T(8,128)}) fusion(pred[512,1024]{1,0:T(8,128)(4,1)} %broadcast_compare_fusion, bf16[512,12,64]{0,2,1:T(8,128)(2,1)S(1)} %bitcast.80, bf16[1024,12,64]{0,2,1:T(8,128)(2,1)S(1)} %bitcast.77), kind=kOutput, calls=%fused_computation.4 | convolution fusion | flops 817883136 | bytes 28073984 | tf_op jit(solution)/shard_map/qhd,khd->hqk/dot_general | solution.py:595
  175.2 11.6 %exponential_reduce_fusion = f32[12,512]{1,0:T(8,128)S(1)} fusion(f32[12,512,1024]{2,1,0:T(8,128)} %get-tuple-element.88, f32[12,512]{1,0:T(8,128)S(1)} %get-tuple-element.87, pred[512,1024]{1,0:T(8,128)(4,1)S(1)} %copy-done.11), kind=kLoop, calls=%fused_computation.2 | loop fusion | flops 18868224 | bytes 25739264 | tf_op jit(solution)/shard_map/reduce_sum | solution.py:682
  186.9 10.9 %fusion.31 = bf16[12,64,512]{2,1,0:T(8,128)(2,1)S(1)} fusion(bf16[1024,12,64]{0,2,1:T(8,128)(2,1)S(1)} %bitcast.89, f32[12,512,1024]{2,1,0:T(8,128)} %get-tuple-element.88, f32[12,512]{1,0:T(8,128)S(1)} %log_add_fusion, pred[512,1024]{1,0:T(8,128)(4,1)S(1)} %copy-done.11), kind=kOutput, calls=%fused_computation.68 | convolution fusion | flops 824573952 | bytes 28073984 | tf_op jit(solution)/shard_map/hqk,khd->qhd/dot_general | solution.py:684
  197.8 0.9 fusion.51
  199.5 1.7 slice-done.2
  201.2 4.5 multiply_convert_fusion.1
  205.8 5.1 %fusion.46 = (f32[3072]{0:T(1024)S(1)}, bf16[512,3072]{1,0:T(8,128)(2,1)S(1)}) fusion(f32[512,3072]{1,0:T(8,128)S(1)} %get-tuple-element.92, f32[3072]{0:T(1024)S(1)} %slice_bitcast_fusion, bf16[512,768]{1,0:T(8,128)(2,1)S(1)} %copy-done.13, bf16[3072,768]{1,0:T(8,128)(2,1)S(1)} %bitcast.92), kind=kOutput, calls=%fused_computation.119 | convolution fusion | flops 2434790400 | bytes 14966784 | tf_op jit(solution)/shard_map/td,fd->tf/dot_general | solution.py:703
  210.9 3.1 multiply_reduce_fusion
  214.7 1.1 copy-done.4
  215.9 0.9 copy-done.17
  216.8 1.7 convolution_convert_fusion
  218.5 1.4 copy.26
  220.2 12.9 %fusion.27 = f32[12,64,1024]{2,1,0:T(8,128)} fusion(bf16[512,12,64]{0,2,1:T(8,128)(2,1)S(1)} %bitcast.83, f32[12,512,1024]{2,1,0:T(8,128)} %get-tuple-element.88, f32[12,512]{1,0:T(8,128)S(1)} %log_add_fusion, pred[512,1024]{1,0:T(8,128)(4,1)S(1)} %copy-done.12), kind=kOutput, calls=%fused_computation.64 | convolution fusion | flops 824180736 | bytes 29646848 | tf_op jit(solution)/shard_map/hqk,qhd->khd/dot_general | solution.py:726
  233.1 16.7 %multiply_convert_fusion = bf16[12,512,1024]{2,1,0:T(8,128)(2,1)} fusion(f32[12,512,1024]{2,1,0:T(8,128)} %get-tuple-element.88, f32[12,512]{1,0:T(8,128)S(1)} %bitcast.90, f32[12,512]{1,0:T(8,128)S(1)} %log_add_fusion, pred[512,1024]{1,0:T(8,128)(4,1)S(1)} %copy-done.12, bf16[512,12,64]{0,2,1:T(8,128)(2,1)S(1)} %bitcast.84, bf16[1024,12,64]{0,2,1:T(8,128)(2,1)} %bitcast.88), kind=kOutput, calls=%fused_computation | convolution fusion | flops 836763648 | bytes 40681472 | tf_op jit(solution)/shard_map/qhd,khd->hqk/dot_general | solution.py:727
  249.7 8.5 %fusion.53 = f32[12,64,1024]{2,1,0:T(8,128)} fusion(bf16[512,12,64]{0,2,1:T(8,128)(2,1)S(1)} %bitcast.81, bf16[12,512,1024]{2,1,0:T(8,128)(2,1)} %multiply_convert_fusion), kind=kOutput, calls=%fused_computation.126 | convolution fusion | flops 805306368 | bytes 16515072 | tf_op jit(solution)/shard_map/hqk,qhd->khd/dot_general | solution.py:740
  258.3 2.4 copy.27
  260.7 3.5 copy.28
  264.2 2.2 fusion.34
  266.4 4.9 collective-permute-start.2
  271.4 29.4 %collective-permute-done.2 = f32[196,1536]{1,0:T(8,128)} collective-permute-done((f32[196,1536]{1,0:T(8,128)}, f32[196,1536]{1,0:T(8,128)}, u32[]{:S(2)}, u32[]{:S(2)}) %collective-permute-start.2) | collective-permute-done | bytes 1204256 | tf_op jit(solution)/shard_map/ppermute | solution.py:554
  300.8 3.4 pad_maximum_fusion.1
  304.2 3.9 collective-permute-start.3
  308.1 9.4 %fusion.49 = (f32[12,64]{1,0:T(8,128)S(1)}, bf16[12,64,512]{2,1,0:T(8,128)(2,1)}) fusion(bf16[1024,12,64]{0,2,1:T(8,128)(2,1)S(1)} %bitcast.78, bf16[12,512,1024]{2,1,0:T(8,128)(2,1)} %multiply_convert_fusion), kind=kOutput, calls=%fused_computation.122 | convolution fusion | flops 806485248 | bytes 14945280 | tf_op jit(solution)/shard_map/hqk,khd->qhd/dot_general | solution.py:736
  317.5 2.3 copy.30.attended
  319.9 2.3 copy.29
  322.2 3.6 fusion.7
  325.9 6.2 %add_select_fusion = f32[512,768]{1,0:T(8,128)} fusion(f32[512,768]{1,0:T(8,128)S(1)} %copy-done.3, bf16[512,3072]{1,0:T(8,128)(2,1)S(1)} %copy-done.21, bf16[3072,768]{1,0:T(8,128)(2,1)} %get-tuple-element.47, f32[768]{0:T(1024)S(1)} %get-tuple-element.77, pred[512]{0:T(512)(128)(4,1)S(1)} %iota_compare_fusion), kind=kOutput, calls=%fused_computation.61 | convolution fusion | flops 2417098752 | bytes 11013632 | tf_op jit(solution)/shard_map/dot_general | solution.py:697
  332.1 3.3 scatter-add.4
  335.4 2.5 dynamic-slice_add_fusion
  337.9 3.3 dynamic_update_slice.3
  341.6 0.8 copy-done.9
  342.6 1.1 copy-done.25
  343.7 2.4 fusion.21
  346.1 1.6 pad_maximum_fusion.joined
  348.4 27.5 %weight_grads.1 = bf16[4,14080,128]{2,1,0:T(8,128)(2,1)} custom-call(bf16[512,768]{1,0:T(8,128)(2,1)} %copy-done.15, bf16[512,2304]{1,0:T(8,128)(2,1)} %pad_maximum_fusion.joined, bf16[512,768]{1,0:T(8,128)(2,1)} %copy.30.attended, bf16[512,768]{1,0:T(8,128)(2,1)} %copy-done.17, bf16[512,768]{1,0:T(8,128)(2,1)} %copy-done.16, bf16[512,3072]{1,0:T(8,128)(2,1)} %copy-done.22, ...), custom_call_target="tpu_custom_call" | custom-call | tf_op jit(solution)/shard_map/weight_grads/pallas_call | solution.py:328
  375.9 103.5 %reduce_grads.1 = bf16[8,2,880,128]{3,2,1,0:T(8,128)(2,1)} custom-call(bf16[4,8,2,880,128]{4,3,2,1,0:T(8,128)(2,1)} %bitcast.71), custom_call_target="tpu_custom_call" | custom-call | tf_op jit(solution)/shard_map/reduce_grads/pallas_call | solution.py:517
  479.5 2.3 slice_convert_fusion
  482.1 4.9 reshape.319
  487.0 1.7 fusion.20
  488.7 0.8 copy-done
  489.6 14.9 %multiply_subtract_fusion = (f32[1771776]{0:T(1024)}, f32[1771776]{0:T(1024)}, f32[1771776]{0:T(1024)}) fusion(f32[1771776]{0:T(1024)} %param.15, s32[]{:T(128)S(6)} %mul.251, bf16[1802240]{0:T(1024)(128)(2,1)S(1)} %bitcast.74, f32[1771776]{0:T(1024)} %param.16, f32[1771776]{0:T(1024)} %param.17), kind=kLoop, calls=%fused_computation.14 | loop fusion | flops 33663744 | bytes 46066180 | tf_op jit(solution)/shard_map/sub | solution.py:803
  (100 shorter events, 5.8 us)
Async XLA Ops:
  90.2 17.1 %copy-start.8 = (bf16[512,768]{1,0:T(8,128)(2,1)S(1)}, bf16[512,768]{1,0:T(8,128)(2,1)}, u32[]{:S(2)}) copy-start(bf16[512,768]{1,0:T(8,128)(2,1)} %param.12) | copy-start | bytes 2359300
  90.3 17.1 %copy-start.24 = (bf16[512,768]{1,0:T(8,128)(2,1)S(1)}, bf16[512,768]{1,0:T(8,128)(2,1)}, u32[]{:S(2)}) copy-start(bf16[512,768]{1,0:T(8,128)(2,1)} %param.13) | copy-start | bytes 2359300
  108.7 4.3 copy-start.15
  113.0 2.2 copy-start.14
  119.4 21.6 %collective-permute-start = (bf16[196,1536]{1,0:T(8,128)(2,1)}, bf16[196,1536]{1,0:T(8,128)(2,1)}, u32[]{:S(2)}, u32[]{:S(2)}) collective-permute-start(bf16[196,1536]{1,0:T(8,128)(2,1)} %get-tuple-element.75), channel_id=1, source_target_pairs={{0,1},{1,2},{2,3},{3,4},{4,5},{5,6},{6,7},{7,8},{8,9},{9,10},{10,1... | collective-permute-start | bytes 1806344 | tf_op jit(solution)/shard_map/ppermute | solution.py:554
  122.6 31.9 %collective-permute-start.1 = (bf16[196,1536]{1,0:T(8,128)(2,1)}, bf16[196,1536]{1,0:T(8,128)(2,1)}, u32[]{:S(2)}, u32[]{:S(2)}) collective-permute-start(bf16[196,1536]{1,0:T(8,128)(2,1)} %get-tuple-element.76), channel_id=1, source_target_pairs={{1,0},{2,1},{3,2},{4,3},{5,4},{6,5},{7,6},{8,7},{9,8},{10,9},{11,1... | collective-permute-start | bytes 1806344 | tf_op jit(solution)/shard_map/ppermute | solution.py:556
  160.7 14.5 %copy-start.6 = (bf16[1024,768]{0,1:T(8,128)(2,1)}, bf16[1024,768]{0,1:T(8,128)(2,1)S(1)}, u32[]{:S(2)}) copy-start(bf16[1024,768]{0,1:T(8,128)(2,1)S(1)} %copy.25) | copy-start | bytes 4718596
  163.9 11.3 %copy-start.11 = (pred[512,1024]{1,0:T(8,128)(4,1)S(1)}, pred[512,1024]{1,0:T(8,128)(4,1)}, u32[]{:S(2)}) copy-start(pred[512,1024]{1,0:T(8,128)(4,1)} %broadcast_compare_fusion) | copy-start | bytes 1572868
  175.2 11.6 %copy-start.23 = (bf16[1024,768]{0,1:T(8,128)(2,1)S(1)}, bf16[1024,768]{0,1:T(8,128)(2,1)}, u32[]{:S(2)}) copy-start(bf16[1024,768]{0,1:T(8,128)(2,1)} %copy.23) | copy-start | bytes 4718596
  186.9 11.0 %copy-start.26 = (bf16[768,768]{1,0:T(8,128)(2,1)S(1)}, bf16[768,768]{1,0:T(8,128)(2,1)}, u32[]{:S(2)}) copy-start(bf16[768,768]{1,0:T(8,128)(2,1)} %get-tuple-element.45) | copy-start | bytes 3538948
  197.8 1.3 copy-start.19
  197.8 3.3 slice-start.2
  197.8 3.4 slice-start.3
  198.8 15.2 %copy-start.2 = (f32[512,768]{1,0:T(8,128)}, f32[512,768]{1,0:T(8,128)S(1)}, u32[]{:S(2)}) copy-start(f32[512,768]{1,0:T(8,128)S(1)} %get-tuple-element.90) | copy-start | bytes 4718596
  199.1 6.6 %slice-start = ((s8[4718592]{0:T(1024)(128)(4,1)}), s8[4194304]{0:T(1024)(128)(4,1)S(1)}, s32[]{:S(2)}) async-start(s8[4718592]{0:T(1024)(128)(4,1)} %bitcast.91), calls=%async_computation | async-start | bytes 8388608
  199.5 6.3 %copy-start.16 = (bf16[512,768]{1,0:T(8,128)(2,1)}, bf16[512,768]{1,0:T(8,128)(2,1)S(1)}, u32[]{:S(2)}) copy-start(bf16[512,768]{1,0:T(8,128)(2,1)S(1)} %add_convert_fusion.feed_two) | copy-start | bytes 2359300
  201.2 4.5 copy-start.13
  201.2 4.5 slice-start.1
  210.9 3.1 copy-start.22
  214.0 2.8 copy-start.27
  214.7 1.1 copy-start.4
  215.9 0.9 copy-start.17
  216.8 3.1 copy-start.20
  216.8 3.4 copy-start.12
  266.4 34.3 %collective-permute-start.2 = (f32[196,1536]{1,0:T(8,128)}, f32[196,1536]{1,0:T(8,128)}, u32[]{:S(2)}, u32[]{:S(2)}) collective-permute-start(f32[196,1536]{1,0:T(8,128)} %fusion.34), channel_id=1, source_target_pairs={{0,1},{1,2},{2,3},{3,4},{4,5},{5,6},{6,7},{7,8},{8,9},{9,10},{10,1... | collective-permute-start | bytes 3612680 | tf_op jit(solution)/shard_map/ppermute | solution.py:554
  271.4 36.7 %copy-start.7 = (bf16[1024,768]{0,1:T(8,128)(2,1)S(1)}, bf16[1024,768]{0,1:T(8,128)(2,1)}, u32[]{:S(2)}) copy-start(bf16[1024,768]{0,1:T(8,128)(2,1)} %copy-done.6) | copy-start | bytes 4718596
  304.2 31.2 %collective-permute-start.3 = (f32[196,1536]{1,0:T(8,128)}, f32[196,1536]{1,0:T(8,128)}, u32[]{:S(2)}, u32[]{:S(2)}) collective-permute-start(f32[196,1536]{1,0:T(8,128)} %get-tuple-element.65), channel_id=1, source_target_pairs={{1,0},{2,1},{3,2},{4,3},{5,4},{6,5},{7,6},{8,7},{9,8},{10,9},{11,1... | collective-permute-start | bytes 3612680 | tf_op jit(solution)/shard_map/ppermute | solution.py:556
  322.2 3.6 copy-start.3
  322.2 3.6 copy-start.21
  325.9 6.2 %copy-start.1 = (f32[512,1536]{1,0:T(8,128)S(1)}, f32[512,1536]{1,0:T(8,128)}, u32[]{:S(2)}) copy-start(f32[512,1536]{1,0:T(8,128)} %fusion.7) | copy-start | bytes 9437188
  341.2 1.1 copy-start.9
  341.2 1.4 copy-start.18
  341.2 2.5 copy-start.25
  481.7 5.2 %copy-start.5 = (f32[512,768]{1,0:T(8,128)S(1)}, f32[512,768]{1,0:T(8,128)}, u32[]{:S(2)}) copy-start(f32[512,768]{1,0:T(8,128)} %copy-done.4) | copy-start | bytes 4718596
  481.8 5.2 %copy-start.10 = (bf16[512,768]{1,0:T(8,128)(2,1)S(1)}, bf16[512,768]{1,0:T(8,128)(2,1)}, u32[]{:S(2)}) copy-start(bf16[512,768]{1,0:T(8,128)(2,1)} %param.12) | copy-start | bytes 2359300
  487.0 2.6 copy-start

commit v2 on v1

--- a/solution.py
+++ b/solution.py
@@ -13,8 +13,6 @@
 FF = 3072
 IMG = 197
 BLOCK = 512
-HALO = 196
-KEY_SPAN = 1024
 
 
 ln_eps = 1e-06
@@ -54,10 +52,11 @@
     return index + sum((1 << b) * (1 - 2 * bits[b]) for b in which)
 
 
-def greet(n_dp, n_shard, place, level, bits):
+def greet(n_dp, n_shard, place, level, bits, extra=()):
     barrier = pltpu.get_barrier_semaphore()
     peers = [(place, lax.rem(level + j, n_shard)) for j in range(1, n_shard)]
     peers += [(flipped(place, bits, [b]), level) for b in range(len(bits))]
+    peers += list(extra)
     for peer in peers:
         pl.semaphore_signal(barrier, inc=1, device_id=peer, device_id_type=MESH)
     pl.semaphore_wait(barrier, len(peers))
@@ -70,12 +69,22 @@
     return found
 
 
-def gather_kernel(n_dp, n_shard, half, own, out, z_send, z_recv, d_send, d_recv):
+def ring(n_dp, n_shard, place, level):
+    spot = place * n_shard + level
+    size = n_dp * n_shard
+    sides = [lax.rem(spot + size - 1, size), lax.rem(spot + 1, size)]
+    return [(lax.div(side, n_shard), lax.rem(side, n_shard)) for side in sides]
+
+
+def gather_kernel(
+    n_dp, n_shard, half, own, head, tail, out, before, after, z_send, z_recv, d_send, d_recv, r_send, r_recv
+):
     place = lax.axis_index("dp")
     level = lax.axis_index("shard")
     count, orders = bit_list(n_dp)
     bits = bits_of(place, count)
-    greet(n_dp, n_shard, place, level, bits)
+    previous, following = ring(n_dp, n_shard, place, level)
+    greet(n_dp, n_shard, place, level, bits, (previous, following))
     started = []
 
     def push(src, dst, send, recv, target):
@@ -90,6 +99,8 @@
         copy.start()
         started.append(copy)
 
+    push(head, after, r_send.at[0], r_recv.at[0], previous)
+    push(tail, before, r_send.at[1], r_recv.at[1], following)
     for side in range(2):
         for j in range(1, n_shard):
             push(
@@ -143,28 +154,37 @@
             chunk = tick - stage
             if 0 <= chunk < len(chunks):
                 advance(chunk, stage)
+    started[0].wait_recv()
+    started[1].wait_recv()
     for copy in started:
         copy.wait_send()
 
 
-def gather_weights(n_dp, n_shard, own):
+def gather_weights(n_dp, n_shard, own, head, tail):
     shard_lines, piece, padded = geometry(n_dp, n_shard)
     half = piece // 2
     chunks = 2 * (n_shard - 1)
+    space = pl.BlockSpec(memory_space=pltpu.HBM)
     return pl.pallas_call(
         functools.partial(gather_kernel, n_dp, n_shard, half),
-        out_shape=jax.ShapeDtypeStruct((n_shard, n_dp, 2, half, LANES), jnp.bfloat16),
-        in_specs=[pl.BlockSpec(memory_space=pltpu.HBM)],
-        out_specs=pl.BlockSpec(memory_space=pltpu.HBM),
+        out_shape=[
+            jax.ShapeDtypeStruct((n_shard, n_dp, 2, half, LANES), jnp.bfloat16),
+            jax.ShapeDtypeStruct((RIM, D), jnp.bfloat16),
+            jax.ShapeDtypeStruct((RIM, D), jnp.bfloat16),
+        ],
+        in_specs=[space] * 3,
+        out_specs=[space] * 3,
         scratch_shapes=[
             pltpu.SemaphoreType.DMA((n_shard - 1, 2)),
             pltpu.SemaphoreType.DMA((n_shard - 1, 2)),
             pltpu.SemaphoreType.DMA((chunks, n_dp - 1)),
             pltpu.SemaphoreType.DMA((chunks, n_dp - 1)),
+            pltpu.SemaphoreType.DMA((2,)),
+            pltpu.SemaphoreType.DMA((2,)),
         ],
         compiler_params=pltpu.CompilerParams(collective_id=1, has_side_effects=True),
         name="gather_weights",
-    )(own)
+    )(own, head, tail)
 
 
 def weight_plan(n_shard, shard_lines):
@@ -543,21 +563,181 @@
     )(grads.reshape(n_shard, n_dp, 2, half, LANES))
 
 
-def extended_2(cells, sides, width):
-    for axis, dim in sides:
-        count = lax.axis_size(axis)
-        ends = count - 1
-        head = lax.slice_in_dim(cells, 0, width, axis=dim)
-        tail = lax.slice_in_dim(cells, cells.shape[dim] - width, cells.shape[dim], axis=dim)
-        cells = jnp.concatenate(
-            [
-                lax.ppermute(tail, axis, [(i, (i + 1) % count) for i in range(ends)]),
-                cells,
-                lax.ppermute(head, axis, [((i + 1) % count, i) for i in range(ends)]),
-            ],
-            axis=dim,
-        )
-    return cells
+RIM = 208
+EXT = 1024
+QB = 128
+WIN = 640
+
+
+def window_bias(start, block):
+    inv = 1.0 / IMG
+    rows = lax.broadcasted_iota(jnp.int32, (QB, 1), 0) + (start + block * QB)
+    cols = lax.broadcasted_iota(jnp.int32, (1, WIN), 1) + (start - RIM + block * QB)
+    row_image = jnp.floor((rows.astype(jnp.float32) + 0.5) * inv)
+    col_image = jnp.floor((cols.astype(jnp.float32) + 0.5) * inv)
+    return jnp.where(row_image == col_image, 0.0, masked)
+
+
+def stacked(rows):
+    lane = lax.broadcasted_iota(jnp.int32, (QB, LANES), 1)
+    zero = jnp.zeros_like(rows)
+    return jnp.concatenate([jnp.where(lane < HD, rows, zero), jnp.where(lane < HD, zero, rows)], axis=0)
+
+
+def unstacked(rows):
+    lane = lax.broadcasted_iota(jnp.int32, (QB, LANES), 1)
+    return jnp.where(lane < HD, rows[:QB], rows[QB:])
+
+
+def attend_kernel(bounds, rows, weight, vectors, feed, queries, keys, values, attended, lse, wide_feed, bias):
+    start = bounds[0, 0]
+    gain, shift = vectors[0:1, :], vectors[1:2, :]
+
+    def norm(i, carry):
+        at = pl.multiple_of(i * 64, 64)
+        x = rows[pl.ds(at, 64), :].astype(jnp.float32)
+        centred = x - jnp.mean(x, axis=-1, keepdims=True)
+        inverse = lax.rsqrt(jnp.mean(centred * centred, axis=-1, keepdims=True) + ln_eps)
+        wide_feed[pl.ds(at, 64), :] = (centred * inverse * gain + shift).astype(jnp.bfloat16)
+        return carry
+
+    lax.fori_loop(0, EXT // 64, norm, 0)
+    feed[...] = wide_feed[RIM : RIM + BLOCK, :]
+
+    def project(i, carry):
+        at = pl.multiple_of(i * 256, 256)
+        block = wide_feed[pl.ds(at, 256), :]
+        keys[pl.ds(at, 256), :] = jnp.dot(
+            block, weight[:, D : 2 * D], preferred_element_type=jnp.float32
+        ).astype(jnp.bfloat16)
+        values[pl.ds(at, 256), :] = (
+            jnp.dot(block, weight[:, 2 * D :], preferred_element_type=jnp.float32) + vectors[3:4, :]
+        ).astype(jnp.bfloat16)
+        return carry
+
+    lax.fori_loop(0, EXT // 256, project, 0)
+
+    def ask(i, carry):
+        at = pl.multiple_of(i * 256, 256)
+        queries[pl.ds(at, 256), :] = (
+            (jnp.dot(feed[pl.ds(at, 256), :], weight[:, :D], preferred_element_type=jnp.float32) + vectors[2:3, :])
+            * 0.125
+        ).astype(jnp.bfloat16)
+        return carry
+
+    lax.fori_loop(0, BLOCK // 256, ask, 0)
+    for block in range(BLOCK // QB):
+        bias[block] = window_bias(start, block)
+
+    def attend(i, carry):
+        block = lax.rem(i, BLOCK // QB)
+        pair = lax.div(i, BLOCK // QB)
+        at = pl.multiple_of(block * QB, QB)
+        lanes = pl.ds(pl.multiple_of(pair * LANES, LANES), LANES)
+        scores = lax.dot_general(
+            stacked(queries[pl.ds(at, QB), lanes]),
+            keys[pl.ds(at, WIN), lanes],
+            (((1,), (1,)), ((), ())),
+            preferred_element_type=jnp.float32,
+        )
+        cover = bias[block]
+        scores = scores + jnp.concatenate([cover, cover], axis=0)
+        top = jnp.max(scores, axis=-1, keepdims=True)
+        raised = jnp.exp(scores - top)
+        total = jnp.sum(raised, axis=-1, keepdims=True)
+        probs = (raised * (1.0 / total)).astype(jnp.bfloat16)
+        out = jnp.dot(probs, values[pl.ds(at, WIN), lanes], preferred_element_type=jnp.float32)
+        attended[pl.ds(at, QB), lanes] = unstacked(out).astype(jnp.bfloat16)
+        lse[pair, block] = jnp.broadcast_to(top + jnp.log(total), (2 * QB, LANES))
+        return carry
+
+    lax.fori_loop(0, HEADS // 2 * (BLOCK // QB), attend, 0)
+
+
+def attend(bounds, rows, weight, vectors):
+    half = jnp.bfloat16
+    return pl.pallas_call(
+        attend_kernel,
+        out_shape=[
+            jax.ShapeDtypeStruct((BLOCK, D), half),
+            jax.ShapeDtypeStruct((BLOCK, D), half),
+            jax.ShapeDtypeStruct((EXT, D), half),
+            jax.ShapeDtypeStruct((EXT, D), half),
+            jax.ShapeDtypeStruct((BLOCK, D), half),
+            jax.ShapeDtypeStruct((HEADS // 2, BLOCK // QB, 2 * QB, LANES), jnp.float32),
+        ],
+        in_specs=[pl.BlockSpec(memory_space=pltpu.SMEM)] + [pl.BlockSpec(memory_space=pltpu.VMEM)] * 3,
+        out_specs=[pl.BlockSpec(memory_space=pltpu.VMEM)] * 6,
+        scratch_shapes=[
+            pltpu.VMEM((EXT, D), half),
+            pltpu.VMEM((BLOCK // QB, QB, WIN), jnp.float32),
+        ],
+        compiler_params=pltpu.CompilerParams(vmem_limit_bytes=60 << 20),
+        name="attend",
+    )(bounds, rows, weight, vectors)
+
+
+def attend_back_kernel(bounds, queries, keys, values, attended, grads, lse, query_grad, key_grad, value_grad, bias):
+    start = bounds[0, 0]
+    for block in range(BLOCK // QB):
+        bias[block] = window_bias(start, block)
+    key_grad[...] = jnp.zeros_like(key_grad)
+    value_grad[...] = jnp.zeros_like(value_grad)
+
+    def body(i, carry):
+        block = lax.rem(i, BLOCK // QB)
+        pair = lax.div(i, BLOCK // QB)
+        at = pl.multiple_of(block * QB, QB)
+        lanes = pl.ds(pl.multiple_of(pair * LANES, LANES), LANES)
+        asked = stacked(queries[pl.ds(at, QB), lanes])
+        own_grad = grads[pl.ds(at, QB), lanes]
+        given = stacked(own_grad)
+        near_keys = keys[pl.ds(at, WIN), lanes]
+        near_values = values[pl.ds(at, WIN), lanes]
+        scores = lax.dot_general(
+            asked, near_keys, (((1,), (1,)), ((), ())), preferred_element_type=jnp.float32
+        )
+        cover = bias[block]
+        level = lse[pair, block]
+        probs = jnp.exp(
+            scores + jnp.concatenate([cover, cover], axis=0) - jnp.concatenate([level] * (WIN // LANES), axis=1)
+        )
+        prob_grad = lax.dot_general(
+            given, near_values, (((1,), (1,)), ((), ())), preferred_element_type=jnp.float32
+        )
+        wide = given.astype(jnp.float32) * jnp.concatenate([attended[pl.ds(at, QB), lanes]] * 2, axis=0).astype(
+            jnp.float32
+        )
+        centre = jnp.sum(wide, axis=-1, keepdims=True)
+        score_grad = (probs * (prob_grad - centre)).astype(jnp.bfloat16)
+        query_grad[pl.ds(at, QB), lanes] = (
+            unstacked(jnp.dot(score_grad, near_keys, preferred_element_type=jnp.float32)) * 0.125
+        )
+        key_grad[pl.ds(at, WIN), lanes] += lax.dot_general(
+            score_grad, asked, (((0,), (0,)), ((), ())), preferred_element_type=jnp.float32
+        )
+        value_grad[pl.ds(at, WIN), lanes] += lax.dot_general(
+            probs.astype(jnp.bfloat16), given, (((0,), (0,)), ((), ())), preferred_element_type=jnp.float32
+        )
+        return carry
+
+    lax.fori_loop(0, HEADS // 2 * (BLOCK // QB), body, 0)
+
+
+def attend_back(bounds, queries, keys, values, attended, grads, lse):
+    return pl.pallas_call(
+        attend_back_kernel,
+        out_shape=[
+            jax.ShapeDtypeStruct((BLOCK, D), jnp.float32),
+            jax.ShapeDtypeStruct((EXT, D), jnp.float32),
+            jax.ShapeDtypeStruct((EXT, D), jnp.float32),
+        ],
+        in_specs=[pl.BlockSpec(memory_space=pltpu.SMEM)] + [pl.BlockSpec(memory_space=pltpu.VMEM)] * 6,
+        out_specs=[pl.BlockSpec(memory_space=pltpu.VMEM)] * 3,
+        scratch_shapes=[pltpu.VMEM((BLOCK // QB, QB, WIN), jnp.float32)],
+        compiler_params=pltpu.CompilerParams(vmem_limit_bytes=60 << 20),
+        name="attend_back",
+    )(bounds, queries, keys, values, attended, grads, lse)
 
 
 def gelu_value(preact):
@@ -569,6 +749,12 @@
         0.5 * (1.0 + lax.erf(preact * sqrt_half))
         + preact * jnp.exp(-0.5 * preact * preact) * inv_root_two_pi
     )
+
+
+def norm_stats(values):
+    centred = values - jnp.mean(values, axis=-1, keepdims=True)
+    inverse = lax.rsqrt(jnp.mean(centred * centred, axis=-1, keepdims=True) + ln_eps)
+    return centred * inverse, inverse
 
 
 def norm_forward(values, gain_vec, shift_vec):
@@ -587,20 +773,6 @@
     return inverse * (scaled - first_mean - normed * second)
 
 
-def split_heads(matrix):
-    return matrix.reshape(matrix.shape[0], HEADS, HD)
-
-
-def block_scores(query_rows, key_rows, allowed):
-    raw = jnp.einsum(
-        "qhd,khd->hqk",
-        split_heads(query_rows),
-        split_heads(key_rows),
-        preferred_element_type=jnp.float32,
-    )
-    return jnp.where(allowed[None], raw, masked)
-
-
 def shards(block_input, cotangent, token_bounds, params, first_moment, second_moment):
     rows_here = block_input.shape[0]
     own_len = params.shape[0]
@@ -609,7 +781,9 @@
     own_weights = jnp.pad(params.astype(jnp.bfloat16), (0, padded * LANES - own_len)).reshape(
         n_dp, 2, piece // 2, LANES
     )
-    gathered = gather_weights(n_dp, n_shard, own_weights)
+    live_count = token_bounds[0, 1] - token_bounds[0, 0]
+    tail_rows = lax.dynamic_slice_in_dim(jnp.pad(block_input, ((16, 0), (0, 0))), live_count + (16 - RIM), RIM, 0)
+    gathered, before, after = gather_weights(n_dp, n_shard, own_weights, block_input[:RIM], tail_rows)
     weight_qkv, weight_out, weight_in, weight_back, lines = lay_out_weights(
         n_dp, n_shard, own_weights, gathered
     )
@@ -617,75 +791,17 @@
     bias_in = lines[8 * D // LANES :].reshape(FF)
     gain_one, shift_one, bias_q, bias_v = (vector_f[0], vector_f[1], vector_f[2], vector_f[3])
     bias_out, gain_two, shift_two, bias_back = (vector_f[4], vector_f[5], vector_f[6], vector_f[7])
-    start_tok = token_bounds[0, 0]
-    stop_tok = token_bounds[0, 1]
-    live_count = stop_tok - start_tok
     slot_ids = jnp.arange(rows_here, dtype=jnp.int32)
     is_live = slot_ids < live_count
-    positions = start_tok + slot_ids
     stream = block_input.astype(jnp.float32)
-    first_out, first_normed, first_inv = norm_forward(stream, gain_one, shift_one)
-    first_feed = first_out.astype(jnp.bfloat16)
-    projected = jnp.dot(first_feed, weight_qkv, preferred_element_type=jnp.float32)
-    queries = ((projected[:, :D] + bias_q) * 0.125).astype(jnp.bfloat16)
-    key_value = jnp.concatenate(
-        [projected[:, D : 2 * D], projected[:, 2 * D :] + bias_v], axis=1
-    ).astype(jnp.bfloat16)
-    rim_rows = jnp.concatenate(
-        [key_value[:HALO], lax.dynamic_slice_in_dim(key_value, live_count - HALO, HALO, 0)], axis=0
-    )
-    rim_pairs = extended_2(rim_rows, ((("dp", "shard"), 0),), HALO)
-    spare_rows = KEY_SPAN - BLOCK - 2 * HALO
-    extended = jnp.concatenate(
-        [
-            rim_pairs[:HALO],
-            key_value,
-            rim_pairs[3 * HALO :],
-            jnp.zeros((spare_rows, 2 * D), jnp.bfloat16),
-        ],
-        axis=0,
-    )
-    cycle_place = lax.axis_index(("dp", "shard"))
-    cycle_last = lax.axis_size(("dp", "shard")) - 1
-    lane_ids = jnp.arange(HALO, dtype=jnp.int32)
-    key_pos = jnp.concatenate(
-        [
-            start_tok - HALO + lane_ids,
-            positions,
-            stop_tok + lane_ids,
-            jnp.zeros((spare_rows,), jnp.int32),
-        ]
-    )
-    key_ok = jnp.concatenate(
-        [
-            jnp.broadcast_to(cycle_place > 0, (HALO,)),
-            is_live,
-            jnp.broadcast_to(cycle_place < cycle_last, (HALO,)),
-            jnp.zeros((spare_rows,), jnp.bool_),
-        ]
-    )
-    key_image = jnp.where(key_ok, key_pos // IMG, -1)
-    query_image = positions // IMG
-
-    def block_view(head_row):
-        allowed = (
-            query_image[head_row : head_row + BLOCK, None]
-            == key_image[None, head_row : head_row + KEY_SPAN]
-        )
-        return (allowed, extended)
-
-    block_num = 0
-    head_row = block_num * BLOCK
-    allowed, key_part = block_view(head_row)
-    scores = block_scores(queries, key_part[:, :D], allowed)
-    row_top = jnp.max(scores, axis=-1, keepdims=True)
-    log_total = row_top + jnp.log(jnp.sum(jnp.exp(scores - row_top), axis=-1, keepdims=True))
-    probs_b = jnp.exp(scores - log_total).astype(jnp.bfloat16)
-    block_out = jnp.einsum(
-        "hqk,khd->qhd", probs_b, split_heads(key_part[:, D:]), preferred_element_type=jnp.float32
-    )
-    attended_list = block_out.reshape(BLOCK, D).astype(jnp.bfloat16)
-    lse_list = [log_total]
+    first_normed, first_inv = norm_stats(stream)
+    wide_rows = jnp.concatenate(
+        [before, block_input, jnp.zeros((EXT - RIM - BLOCK, D), jnp.bfloat16)], axis=0
+    )
+    wide_rows = lax.dynamic_update_slice_in_dim(wide_rows, after, RIM + live_count, 0)
+    first_feed, queries, keys, values, attended_list, lse = attend(
+        token_bounds, wide_rows, weight_qkv, vector_f
+    )
     middle = (
         stream + jnp.dot(attended_list, weight_out, preferred_element_type=jnp.float32) + bias_out
     )
@@ -714,45 +830,26 @@
     attended_grad = jnp.einsum(
         "te,de->td", middle_feed, weight_out, preferred_element_type=jnp.float32
     ).astype(jnp.bfloat16)
-    ext_grad = jnp.zeros((rows_here + KEY_SPAN - BLOCK, 2 * D), jnp.float32)
-    block_num = 0
-    head_row = block_num * BLOCK
-    allowed, key_part = block_view(head_row)
-    scores = block_scores(queries, key_part[:, :D], allowed)
-    probs_f = jnp.exp(scores - lse_list[block_num])
-    probs_b = probs_f.astype(jnp.bfloat16)
-    grad_part = split_heads(attended_grad)
-    value_part = split_heads(key_part[:, D:])
-    value_grad = jnp.einsum("hqk,qhd->khd", probs_b, grad_part, preferred_element_type=jnp.float32)
-    prob_grad = jnp.einsum(
-        "qhd,khd->hqk", grad_part, value_part, preferred_element_type=jnp.float32
-    )
-    centre_term = jnp.sum(
-        grad_part.astype(jnp.float32) * split_heads(attended_list).astype(jnp.float32), axis=-1
-    )
-    score_grad = (probs_f * (prob_grad - jnp.transpose(centre_term)[:, :, None])).astype(
-        jnp.bfloat16
-    )
-    block_qgrad = jnp.einsum(
-        "hqk,khd->qhd", score_grad, split_heads(key_part[:, :D]), preferred_element_type=jnp.float32
-    )
-    query_grads = block_qgrad.reshape(BLOCK, D) * 0.125
-    key_grad = jnp.einsum(
-        "hqk,qhd->khd", score_grad, split_heads(queries), preferred_element_type=jnp.float32
-    )
-    ext_grad = ext_grad.at[head_row : head_row + KEY_SPAN].add(
-        jnp.concatenate([key_grad.reshape(KEY_SPAN, D), value_grad.reshape(KEY_SPAN, D)], axis=1)
-    )
-    outgoing = jnp.concatenate(
-        [ext_grad[:HALO], ext_grad[HALO + rows_here : 2 * HALO + rows_here]], axis=0
-    )
-    incoming = extended_2(outgoing, ((("dp", "shard"), 0),), HALO)
-    own_grad = ext_grad[HALO : HALO + rows_here]
-    own_grad = own_grad.at[:HALO].add(incoming[:HALO])
-    tail_now = lax.dynamic_slice_in_dim(own_grad, live_count - HALO, HALO, 0)
-    own_grad = lax.dynamic_update_slice_in_dim(
-        own_grad, tail_now + incoming[3 * HALO :], live_count - HALO, 0
-    )
+    query_grads, key_ext, value_ext = attend_back(
+        token_bounds, queries, keys, values, attended_list, attended_grad, lse
+    )
+    ext_grad = jnp.concatenate([key_ext, value_ext], axis=1)
+    device_count = n_dp * n_shard
+    forward = [(i, (i + 1) % device_count) for i in range(device_count)]
+    backward = [((i + 1) % device_count, i) for i in range(device_count)]
+    from_after = lax.ppermute(ext_grad[:RIM], ("dp", "shard"), backward)
+    from_before = lax.ppermute(
+        lax.dynamic_slice_in_dim(ext_grad, RIM + live_count, RIM, 0), ("dp", "shard"), forward
+    )
+    spot = lax.axis_index(("dp", "shard"))
+    from_before = jnp.where((spot > 0), from_before, 0.0)
+    from_after = jnp.where((spot < device_count - 1), from_after, 0.0)
+    own_grad = jnp.where(is_live[:, None], ext_grad[RIM : RIM + BLOCK], 0.0)
+    own_grad = own_grad.at[:RIM].add(from_before)
+    own_grad = jnp.pad(own_grad, ((16, 0), (0, 0)))
+    at = live_count + 16 - RIM
+    tail_now = lax.dynamic_slice_in_dim(own_grad, at, RIM, 0)
+    own_grad = lax.dynamic_update_slice_in_dim(own_grad, tail_now + from_after, at, 0)[16:]
     grad_bias_q = jnp.sum(query_grads, axis=0)
     grad_bias_v = jnp.sum(own_grad[:, D:], axis=0)
     joined = jnp.concatenate([query_grads, own_grad], axis=1).astype(jnp.bfloat16)

time: 510 us -> 449 us (0.88)
  matrix products: 97.9 us -> 25.9 us
  Pallas kernels: 224 us -> 284 us
  other arithmetic: 63.2 us -> 33.7 us
  starting transfers between devices: 18 us -> 4.89 us
  waiting for transfers between devices: 49.8 us -> 61.2 us
  local copies, waits for them, and re-layouts: 48 us -> 36.6 us
    dot_general x7 -> x0, matrix products: 74 us -> none  [the longest x1 16.7 us: shards(): jnp.einsum('qhd,khd->hqk', grad_part, value_part, preferred_element_type=...]
    pallas_call x0 -> x2, Pallas kernels: none -> 54 us  [the longest x1 30.4 us: attend(): pl.pallas_call(attend_kernel, out_shape=[jax.ShapeDtypeStruct((BLOCK, D),...]
    pallas_call x1, Pallas kernels: 77 us -> 91.1 us  [gather_weights(): pl.pallas_call(functools.partial(gather_kernel, n_dp, n_shard, half), out...]
    ppermute x4 -> x2, starting transfers between devices: 18 us -> 4.89 us  [the longest x1 4.89 us: shards(): from_after = lax.ppermute(ext_grad[:RIM], ('dp', 'shard'), backward)]
    concatenate x5 -> x1, other arithmetic: 13.1 us -> 0.28 us  [shards(): jnp.concatenate([before, block_input, jnp.zeros((EXT - RIM - BLOCK, D), j...]
    reduce_sum x3, other arithmetic: 13.2 us -> 0.69 us  [the longest x1 0.35 us: norm_stats(): jnp.mean(centred * centred, axis=-1, keepdims=True) + ln_eps]
    ppermute x4 -> x2, waiting for transfers between devices: 49.8 us -> 61.2 us  [the longest x1 61.2 us: shards(): lax.ppermute(lax.dynamic_slice_in_dim(ext_grad, RIM + live_count, RIM, 0)...]
    pallas_call x1, Pallas kernels: 104 us -> 95 us  [reduce_grads(): pl.pallas_call(functools.partial(reduce_kernel, n_dp, n_shard, half), out...]
  transfers between devices with their start and end apart: 4 -> 2, of which waited for: 3 -> 1; matrix products, arithmetic and copies ran while one was open for 6% -> 2% of each run, Pallas kernels for 0% -> 0%
where the time goes in v2:
time: 449 us; the launch traced here: 448 us
  Pallas kernels  284 us (63%)
  waiting for transfers between devices  61.2 us (14%)
  local copies, waits for them, and re-layouts  36.6 us (8%)
  other arithmetic  33.7 us (8%)
  matrix products  25.9 us (6%)
  starting transfers between devices  4.89 us (1%)
    pallas_call x1, Pallas kernels, reduce_grads(): pl.pallas_call(functools.partial(reduce_kernel, n_dp, n_shard, half), out...  95 us
    pallas_call x1, Pallas kernels, gather_weights(): pl.pallas_call(functools.partial(gather_kernel, n_dp, n_shard, half), out...  91.1 us
    ppermute x1, waiting for transfers between devices, shards(): lax.ppermute(lax.dynamic_slice_in_dim(ext_grad, RIM + live_count, RIM, 0)...  61.2 us
    pallas_call x1, Pallas kernels, attend(): pl.pallas_call(attend_kernel, out_shape=[jax.ShapeDtypeStruct((BLOCK, D),...  30.4 us
    pallas_call x1, Pallas kernels, weight_grads(): pl.pallas_call(functools.partial(weight_grad_kernel, n_shard, shard_lines...  27.5 us
    pallas_call x1, Pallas kernels, attend_back(): pl.pallas_call(attend_back_kernel, out_shape=[jax.ShapeDtypeStruct((BLOCK...  23.6 us
    pallas_call x1, Pallas kernels, lay_out_weights(): pl.pallas_call(functools.partial(layout_kernel, n_shard, shard_lines, pad...  16.2 us
    sub x1, other arithmetic, shards(): params - learn_rate * (first_hat / (jnp.sqrt(second_hat) + adam_eps) + de...  14.7 us
  transfers between devices with their start and end apart: 2, of which 1 were waited for; matrix products, arithmetic and copies ran while one was open for 2% of the time, Pallas kernels for 0%

profile of v2, /device:TPU:1, one launch (start us, length us, event | category | flops | bytes accessed | tf_op | source)
XLA Modules:
  0.0 448.5 jit_solution(8347409806454073428)
XLA Ops:
  0.6 1.3 fusion.26
  3.3 3.3 convert_element_type.36
  6.6 0.0 copy-start.1
  6.6 3.8 pad_bitcast_fusion
  10.4 0.9 pad_dynamic-slice_fusion
  11.3 91.1 %gather_weights.1 = (bf16[4,8,2,880,128]{4,3,2,1,0:T(8,128)(2,1)}, bf16[208,768]{1,0:T(8,128)(2,1)}, bf16[208,768]{1,0:T(8,128)(2,1)}) custom-call(bf16[8,2,880,128]{3,2,1,0:T(8,128)(2,1)} %bitcast.38, bf16[208,768]{1,0:T(8,128)(2,1)} %get-tuple-element.76.head, bf16[208,768]{1,0:T(8,128)(2,1)} %get-tuple-element.75.tail), custom_call_target="tpu_custom_call" | custom-call | tf_op jit(solution)/shard_map/gather_weights/pallas_call | solution.py:168
  102.4 16.2 %lay_out_weights.1 = (bf16[768,2304]{1,0:T(8,128)(2,1)}, bf16[768,768]{1,0:T(8,128)(2,1)}, bf16[768,3072]{1,0:T(8,128)(2,1)}, bf16[3072,768]{1,0:T(8,128)(2,1)}, f32[72,128]{1,0:T(8,128)}) custom-call(bf16[14080,128]{1,0:T(8,128)(2,1)} %get-tuple-element.71.own, bf16[4,14080,128]{2,1,0:T(8,128)(2,1)} %bitcast.37), custom_call_target="tpu_custom_call" | custom-call | tf_op jit(solution)/shard_map/lay_out_weights/pallas_call | solution.py:258
  118.6 0.7 slice_bitcast_fusion
  119.3 0.8 slice_bitcast_fusion.1
  120.1 0.7 slice.79
  120.9 0.6 reshape.120.vectors
  121.5 0.1 pad.23.clone
  121.6 0.3 maximum_maximum_fusion
  121.9 1.9 dynamic_update_slice.6.rows
  123.7 0.0 copy-start.6
  123.7 1.1 copy-done.6
  124.9 30.4 %attend.1 = (bf16[512,768]{1,0:T(8,128)(2,1)}, bf16[512,768]{1,0:T(8,128)(2,1)}, bf16[1024,768]{1,0:T(8,128)(2,1)}, bf16[1024,768]{1,0:T(8,128)(2,1)}, bf16[512,...) custom-call(s32[1,2]{1,0:T(1,128)} %bounds.3, bf16[1024,768]{1,0:T(8,128)(2,1)} %copy-done.6, ...), custom_call_target="tpu_custom_call" | custom-call | tf_op jit(solution)/shard_map/attend/pallas_call | solution.py:659
  155.3 2.4 fusion.27
  157.8 0.3 multiply_reduce_fusion.2
  158.1 0.3 convert_reduce_fusion.1
  158.4 0.3 add_convert_fusion.feed_two
  158.7 0.0 slice-start.1
  158.7 6.7 %multiply_convert_fusion = (bf16[512,3072]{1,0:T(8,128)(2,1)}, f32[512,3072]{1,0:T(8,128)S(1)}) fusion(f32[3072]{0:T(1024)S(1)} %slice_bitcast_fusion, bf16[512,768]{1,0:T(8,128)(2,1)S(1)} %add_convert_fusion.feed_two, bf16[768,3072]{1,0:T(8,128)(2,1)} %get-tuple-element.42), kind=kOutput, calls=%fused_computation.11 | convolution fusion | flops 2425356288 | bytes 14954496 | tf_op jit(solution)/shard_map/dot_general | solution.py:810
  165.5 0.0 slice-start.5
  165.5 4.8 %fusion.23 = (f32[3072]{0:T(1024)S(1)}, bf16[512,3072]{1,0:T(8,128)(2,1)S(1)}) fusion(f32[512,3072]{1,0:T(8,128)S(1)} %get-tuple-element.87, f32[3072]{0:T(1024)S(1)} %slice_bitcast_fusion, bf16[512,768]{1,0:T(8,128)(2,1)S(1)} %get-tuple-element.64.tangent, bf16[3072,768]{1,0:T(8,128)(2,1)S(1)} %bitcast.40), kind=kOutput, calls=%fused_computation.73 | convolution fusion | flops 2434790400 | bytes 14966784 | tf_op jit(solution)/shard_map/td,fd->tf/dot_general | solution.py:819
  170.3 3.0 multiply_reduce_fusion
  173.4 0.7 fusion.22
  174.0 1.1 copy-done.2
  175.2 0.1 convert_element_type.41.middle
  175.3 1.7 convolution_convert_fusion.grads
  177.0 23.6 %attend_back.1 = (f32[512,768]{1,0:T(8,128)}, f32[1024,768]{1,0:T(8,128)}, f32[1024,768]{1,0:T(8,128)}) custom-call(s32[1,2]{1,0:T(1,128)} %bounds.3, bf16[512,768]{1,0:T(8,128)(2,1)} %get-tuple-element.44.queries, bf16[1024,768]{1,0:T(8,128)(2,1)} %get-tuple-element.45.keys, bf16[1024,768]{1,0:T(8,128)(2,1)} %get-tuple-element.46.values, ...), custom_call_target="tpu_custom_call" | custom-call | tf_op jit(solution)/shard_map/attend_back/pallas_call | solution.py:728
  200.5 2.5 constant_dynamic-update-slice_fusion.1
  203.1 0.3 copy-done.10
  203.4 0.5 constant_dynamic-update-slice_fusion
  203.8 0.0 copy-start.4
  203.8 2.7 copy-done.4
  206.5 1.7 fusion.24
  208.2 4.9 %collective-permute-start.1 = (f32[208,1536]{1,0:T(8,128)}, f32[208,1536]{1,0:T(8,128)}, u32[]{:S(2)}, u32[]{:S(2)}) collective-permute-start(f32[208,1536]{1,0:T(8,128)} %get-tuple-element.69), channel_id=1, source_target_pairs={{1,0},{2,1},{3,2},{4,3},{5,4},{6,5},{7,6},{8,7},{9,8},{10,9},{11,1... | collective-permute-start | bytes 3833864 | tf_op jit(solution)/shard_map/ppermute | solution.py:840
  213.1 0.2 convert_reduce_fusion
  213.4 3.8 add_select_fusion
  217.1 0.4 fusion.17
  217.5 0.2 fusion.25
  217.7 2.2 slice_select_fusion
  219.9 61.2 %collective-permute-done = f32[208,1536]{1,0:T(8,128)} collective-permute-done((f32[208,1536]{1,0:T(8,128)}, f32[208,1536]{1,0:T(8,128)}, u32[]{:S(2)}, u32[]{:S(2)}) %collective-permute-start) | collective-permute-done | bytes 1277984 | tf_op jit(solution)/shard_map/ppermute | solution.py:841
  281.1 1.7 fusion.19
  282.8 2.0 pad.16
  284.8 1.5 select_add_fusion
  286.3 4.3 dynamic_update_slice.7
  290.6 1.5 slice_reduce_fusion
  292.2 2.1 slice.115
  294.2 1.6 pad_maximum_fusion.joined
  295.8 1.3 copy-done.7
  297.1 3.4 fusion.16
  300.5 0.1 stack.35
  300.6 0.6 maximum_bitcast_fusion.vec
  301.2 27.5 %weight_grads.1 = bf16[4,14080,128]{2,1,0:T(8,128)(2,1)} custom-call(bf16[512,768]{1,0:T(8,128)(2,1)} %get-tuple-element.51.feed_one, bf16[512,2304]{1,0:T(8,128)(2,1)} %pad_maximum_fusion.joined, bf16[512,768]{1,0:T(8,128)(2,1)} %get-tuple-element.40.attended, bf16[512,768]{1,0:T(8,128)(2,1)} %copy-done.9, bf16[512,768]{1,0:T(8,128)(2,1)} %copy-done.8, ...), custom_call_target="tpu_custom_call" | custom-call | tf_op jit(solution)/shard_map/weight_grads/pallas_call | solution.py:348
  328.7 95.0 %reduce_grads.1 = bf16[8,2,880,128]{3,2,1,0:T(8,128)(2,1)} custom-call(bf16[4,8,2,880,128]{4,3,2,1,0:T(8,128)(2,1)} %bitcast.34), custom_call_target="tpu_custom_call" | custom-call | tf_op jit(solution)/shard_map/reduce_grads/pallas_call | solution.py:537
  423.7 2.3 slice_convert_fusion
  426.0 0.0 copy-start.3
  426.0 0.3 dynamic_slice.15
  426.3 4.9 %reshape.125 = f32[1,1,221472]{2,1,0:T(1,128)} reshape(f32[221472]{0:T(1024)S(1)} %dynamic_slice.15) | data formatting | bytes 1771776 | tf_op jit(solution)/shard_map/reshape | solution.py:903
  431.2 1.8 fusion.15
  433.0 0.8 copy-done
  433.8 14.7 %multiply_subtract_fusion = (f32[1771776]{0:T(1024)}, f32[1771776]{0:T(1024)}, f32[1771776]{0:T(1024)}) fusion(f32[1771776]{0:T(1024)} %param.11, s32[]{:T(128)S(6)} %mul.218, bf16[1802240]{0:T(1024)(128)(2,1)S(1)} %bitcast.36, f32[1771776]{0:T(1024)} %param.12, f32[1771776]{0:T(1024)} %param.13), kind=kLoop, calls=%fused_computation.3 | loop fusion | flops 33663744 | bytes 46066180 | tf_op jit(solution)/shard_map/sub | solution.py:900
  (61 shorter events, 0.2 us)
Async XLA Ops:
  6.6 3.8 copy-start.1
  102.4 19.2 %copy-start.16 = (bf16[208,768]{1,0:T(8,128)(2,1)S(1)}, bf16[208,768]{1,0:T(8,128)(2,1)}, u32[]{:S(2)}) copy-start(bf16[208,768]{1,0:T(8,128)(2,1)} %get-tuple-element.35) | copy-start | bytes 958468
  102.4 19.4 %copy-start.17 = (bf16[208,768]{1,0:T(8,128)(2,1)S(1)}, bf16[208,768]{1,0:T(8,128)(2,1)}, u32[]{:S(2)}) copy-start(bf16[208,768]{1,0:T(8,128)(2,1)} %get-tuple-element.36) | copy-start | bytes 958468
  123.7 1.1 copy-start.6
  155.3 2.8 copy-start.15
  158.4 15.0 %copy-start.5 = (bf16[512,768]{1,0:T(8,128)(2,1)}, bf16[512,768]{1,0:T(8,128)(2,1)S(1)}, u32[]{:S(2)}) copy-start(bf16[512,768]{1,0:T(8,128)(2,1)S(1)} %get-tuple-element.64.tangent) | copy-start | bytes 2359300
  158.4 7.1 %slice-start = ((s8[4718592]{0:T(1024)(128)(4,1)}), s8[4194304]{0:T(1024)(128)(4,1)S(1)}, s32[]{:S(2)}) async-start(s8[4718592]{0:T(1024)(128)(4,1)} %bitcast.39), calls=%async_computation | async-start | bytes 8388608
  158.7 6.8 %copy-start.8 = (bf16[512,768]{1,0:T(8,128)(2,1)}, bf16[512,768]{1,0:T(8,128)(2,1)S(1)}, u32[]{:S(2)}) copy-start(bf16[512,768]{1,0:T(8,128)(2,1)S(1)} %add_convert_fusion.feed_two) | copy-start | bytes 2359300
  158.7 6.8 %slice-start.1 = ((s8[4718592]{0:T(1024)(128)(4,1)}), s8[524288]{0:T(1024)(128)(4,1)S(1)}, s32[]{:S(2)}) async-start(s8[4718592]{0:T(1024)(128)(4,1)} %bitcast.39), calls=%async_computation.1 | async-start | bytes 1048576
  158.7 11.6 %slice-start.4 = ((s8[4718592]{0:T(1024)(128)(4,1)}), s8[4194304]{0:T(1024)(128)(4,1)S(1)}, s32[]{:S(2)}) async-start(s8[4718592]{0:T(1024)(128)(4,1)} %bitcast.43), calls=%async_computation.4 | async-start | bytes 8388608
  165.5 4.8 %slice-start.5 = ((s8[4718592]{0:T(1024)(128)(4,1)}), s8[524288]{0:T(1024)(128)(4,1)S(1)}, s32[]{:S(2)}) async-start(s8[4718592]{0:T(1024)(128)(4,1)} %bitcast.43), calls=%async_computation.5 | async-start | bytes 1048576
  170.3 3.0 copy-start.12
  173.4 1.9 copy-start.18
  174.0 1.1 copy-start.2
  175.3 25.3 %copy-start.9 = (bf16[512,768]{1,0:T(8,128)(2,1)}, bf16[512,768]{1,0:T(8,128)(2,1)S(1)}, u32[]{:S(2)}) copy-start(bf16[512,768]{1,0:T(8,128)(2,1)S(1)} %convert_element_type.41.middle) | copy-start | bytes 2359300
  200.5 2.8 copy-start.10
  200.5 12.8 %slice-start.2 = ((s8[4718592]{0:T(1024)(128)(4,1)}), s8[4194304]{0:T(1024)(128)(4,1)S(1)}, s32[]{:S(2)}) async-start(s8[4718592]{0:T(1024)(128)(4,1)} %bitcast.41), calls=%async_computation.2 | async-start | bytes 8388608
  203.4 10.0 %slice-start.3 = ((s8[4718592]{0:T(1024)(128)(4,1)}), s8[524288]{0:T(1024)(128)(4,1)S(1)}, s32[]{:S(2)}) async-start(s8[4718592]{0:T(1024)(128)(4,1)} %bitcast.41), calls=%async_computation.3 | async-start | bytes 1048576
  203.8 2.7 copy-start.4
  206.5 6.8 %copy-start.11 = (bf16[512,3072]{1,0:T(8,128)(2,1)S(1)}, bf16[512,3072]{1,0:T(8,128)(2,1)}, u32[]{:S(2)}) copy-start(bf16[512,3072]{1,0:T(8,128)(2,1)} %get-tuple-element.86.activated) | copy-start | bytes 9437188
  208.2 76.6 %collective-permute-start.1 = (f32[208,1536]{1,0:T(8,128)}, f32[208,1536]{1,0:T(8,128)}, u32[]{:S(2)}, u32[]{:S(2)}) collective-permute-start(f32[208,1536]{1,0:T(8,128)} %get-tuple-element.69), channel_id=1, source_target_pairs={{1,0},{2,1},{3,2},{4,3},{5,4},{6,5},{7,6},{8,7},{9,8},{10,9},{11,1... | collective-permute-start | bytes 3833864 | tf_op jit(solution)/shard_map/ppermute | solution.py:840
  213.1 68.0 %collective-permute-start = (f32[208,1536]{1,0:T(8,128)}, f32[208,1536]{1,0:T(8,128)}, u32[]{:S(2)}, u32[]{:S(2)}) collective-permute-start(f32[208,1536]{1,0:T(8,128)} %get-tuple-element.70), channel_id=1, source_target_pairs={{0,1},{1,2},{2,3},{3,4},{4,5},{5,6},{6,7},{7,8},{8,9},{9,10},{10,1... | collective-permute-start | bytes 3833864 | tf_op jit(solution)/shard_map/ppermute | solution.py:841
  213.3 4.1 copy-start.13
  294.2 2.9 copy-start.7
  426.0 5.2 %copy-start.3 = (f32[512,768]{1,0:T(8,128)S(1)}, f32[512,768]{1,0:T(8,128)}, u32[]{:S(2)}) copy-start(f32[512,768]{1,0:T(8,128)} %copy-done.2) | copy-start | bytes 4718596
  426.0 5.2 %copy-start.14 = (f32[512,768]{1,0:T(8,128)S(1)}, f32[512,768]{1,0:T(8,128)}, u32[]{:S(2)}) copy-start(f32[512,768]{1,0:T(8,128)} %get-tuple-element.90) | copy-start | bytes 4718596
  431.2 2.6 copy-start

commit v3 on v2

--- a/solution.py
+++ b/solution.py
@@ -34,8 +34,7 @@
 def geometry(n_dp, n_shard):
     total = 4 * D * D + 2 * D * FF + 8 * D + FF
     shard_lines = total // n_shard // LANES
-    piece = -(-shard_lines // n_dp // 32) * 32
-    piece = -(-(-(-shard_lines // n_dp)) // 32) * 32
+    piece = -(-(-(-shard_lines // n_dp)) // 64) * 64
     return shard_lines, piece, piece * n_dp
 
 
@@ -271,298 +270,6 @@
     )(own.reshape(padded, LANES), got.reshape(n_shard, padded, LANES))
 
 
-def weight_grad_kernel(
-    n_shard, shard_lines, padded, feed_one, joined, attended, middle, feed_two, slope, activated, tangent, vec, out, wide, narrow, sem
-):
-    lefts = [feed_one, attended, feed_two, activated]
-    rights = [joined, middle, slope, tangent]
-    sizes = [(D, 3 * D), (D, D), (D, FF), (FF, D)]
-    cursor = 0
-    plan = [[] for _ in range(n_shard)]
-    for which, (rows, columns) in enumerate(sizes):
-        width = columns // LANES
-        for s in range(n_shard):
-            begin, stop = s * shard_lines, (s + 1) * shard_lines
-            first = max(0, (begin - cursor) // width)
-            last = min(rows, -(-(stop - cursor) // width))
-            if last > first:
-                first = first // 128 * 128
-                plan[s].append((which, first, last, width, cursor - begin))
-        cursor += rows * width
-    tail = cursor - (n_shard - 1) * shard_lines
-
-    def product(which, row, width, group):
-        return lax.dot_general(
-            lefts[which][:, pl.ds(row, 128)],
-            rights[which][:, group * 768 : (group + 1) * 768],
-            (((0,), (0,)), ((), ())),
-            preferred_element_type=jnp.float32,
-        )
-
-    for s in range(n_shard):
-        for which, first, last, width, offset in plan[s]:
-            full = (last - first) // 128
-
-            def block(i, carry):
-                row = pl.multiple_of(first + i * 128, 128)
-                line = MARGIN + offset + row * width
-                for group in range(width // 6):
-                    tile = product(which, row, width, group)
-                    for c in range(6):
-                        wide[pl.ds(line + group * 6 + c, 128, stride=width), :] = tile[
-                            :, c * LANES : (c + 1) * LANES
-                        ]
-                return carry
-
-            if full:
-                lax.fori_loop(0, full, block, 0)
-            row = first + full * 128
-            rest = -(-(last - row) // 8) * 8
-            if rest:
-                line = MARGIN + offset + row * width
-                for group in range(width // 6):
-                    tile = product(which, row, width, group)
-                    for c in range(6):
-                        wide[pl.ds(line + group * 6 + c, rest, stride=width), :] = tile[
-                            :rest, c * LANES : (c + 1) * LANES
-                        ]
-        if s == n_shard - 1:
-            wide[MARGIN + tail : MARGIN + tail + vec.shape[0], :] = vec[...]
-        slot = s % 2
-        if s >= 2:
-            pltpu.make_async_copy(narrow.at[slot], out.at[s - 2], sem.at[slot]).wait()
-
-        def pack(i, carry):
-            at = pl.multiple_of(i * 128, 128)
-            narrow[slot, pl.ds(at, 128), :] = wide[pl.ds(MARGIN + at, 128), :].astype(jnp.bfloat16)
-            return carry
-
-        lax.fori_loop(0, padded // 128, pack, 0)
-        pltpu.make_async_copy(narrow.at[slot], out.at[s], sem.at[slot]).start()
-    for s in range(n_shard - 2, n_shard):
-        pltpu.make_async_copy(narrow.at[s % 2], out.at[s], sem.at[s % 2]).wait()
-
-
-def weight_grads(n_dp, n_shard, *operands):
-    shard_lines, piece, padded = geometry(n_dp, n_shard)
-    return pl.pallas_call(
-        functools.partial(weight_grad_kernel, n_shard, shard_lines, padded),
-        out_shape=jax.ShapeDtypeStruct((n_shard, padded, LANES), jnp.bfloat16),
-        in_specs=[pl.BlockSpec(memory_space=pltpu.VMEM)] * 9,
-        out_specs=pl.BlockSpec(memory_space=pltpu.HBM),
-        scratch_shapes=[
-            pltpu.VMEM((MARGIN + padded + 128, LANES), jnp.float32),
-            pltpu.VMEM((2, padded, LANES), jnp.bfloat16),
-            pltpu.SemaphoreType.DMA((2,)),
-        ],
-        compiler_params=pltpu.CompilerParams(vmem_limit_bytes=60 << 20),
-        name="weight_grads",
-    )(*operands)
-
-
-def reduce_kernel(n_dp, n_shard, half, grads, out, *scratch):
-    count, orders = bit_list(n_dp)
-    acc, got_core = scratch[0], scratch[1]
-    got_bits = scratch[2 : 1 + count]
-    got_z, final = scratch[1 + count : 3 + count]
-    load_sem, core_send, core_recv, bit_send, bit_recv, z_send, z_recv, g_send, g_recv, keep_sem = scratch[
-        3 + count :
-    ]
-    place = lax.axis_index("dp")
-    level = lax.axis_index("shard")
-    bits = bits_of(place, count)
-    pairs = n_dp // 2
-    chunks = [(j, side) for j in list(range(1, n_shard)) + [0] for side in range(2)]
-    step = 176 if half % 176 == 0 else 32
-    greet(n_dp, n_shard, place, level, bits)
-    started = []
-
-    def push(src, dst, send, recv, target):
-        copy = pltpu.make_async_remote_copy(
-            src_ref=src,
-            dst_ref=dst,
-            send_sem=send,
-            recv_sem=recv,
-            device_id=target,
-            device_id_type=MESH,
-        )
-        copy.start()
-        started.append(copy)
-
-    def landed(buffer, sem):
-        pltpu.make_async_remote_copy(
-            src_ref=buffer,
-            dst_ref=buffer,
-            send_sem=z_send.at[0, 0],
-            recv_sem=sem,
-            device_id=(place, level),
-            device_id_type=MESH,
-        ).wait_recv()
-
-    core = bits[0]
-    partner = flipped(place, bits, [0])
-    for chunk, (j, side) in enumerate(chunks):
-        target = lax.rem(level + j, n_shard)
-        for m in range(pairs):
-            push(
-                grads.at[target, 2 * m + 1 - core, side],
-                got_core.at[chunk, m],
-                core_send.at[chunk, m],
-                core_recv.at[chunk, m],
-                (partner, level),
-            )
-            pltpu.make_async_copy(
-                grads.at[target, 2 * m + core, side], acc.at[chunk, m], load_sem.at[chunk, m]
-            ).start()
-
-    def add(into, other):
-        def body(i, carry):
-            at = pl.multiple_of(i * step, 16)
-            total = into[pl.ds(at, step), :].astype(jnp.float32) + other[pl.ds(at, step), :].astype(
-                jnp.float32
-            )
-            into[pl.ds(at, step), :] = total.astype(jnp.bfloat16)
-            return carry
-
-        lax.fori_loop(0, half // step, body, 0)
-
-    def members(order, stage, flip):
-        fixed = order[:stage]
-        base = sum((bits[b] if b != flip else 1 - bits[b]) * (1 << (b - 1)) for b in fixed)
-        return [base + sum(1 << (b - 1) for b in which) for which in subsets(order[stage:])]
-
-    def advance(chunk, stage):
-        j, side = chunks[chunk]
-        order = orders[side]
-        if stage == 0:
-            for m in range(pairs):
-                pltpu.make_async_copy(
-                    grads.at[0, 2 * m + core, side], acc.at[chunk, m], load_sem.at[chunk, m]
-                ).wait()
-                landed(got_core.at[chunk, m], core_recv.at[chunk, m])
-                add(acc.at[chunk, m], got_core.at[chunk, m])
-        else:
-            for slot, m in enumerate(members(order, stage, None)):
-                buffer = got_bits[stage - 1].at[chunk, slot]
-                landed(buffer, bit_recv.at[stage - 1, chunk, slot])
-                add(acc.at[chunk, m], buffer)
-        if stage < count - 1:
-            flip = order[stage]
-            target = flipped(place, bits, [flip])
-            for slot, m in enumerate(members(order, stage + 1, flip)):
-                push(
-                    acc.at[chunk, m],
-                    got_bits[stage].at[chunk, slot],
-                    bit_send.at[stage, chunk, slot],
-                    bit_recv.at[stage, chunk, slot],
-                    (target, level),
-                )
-        elif j:
-            (m,) = members(order, stage, None)
-            push(
-                acc.at[chunk, m],
-                got_z.at[j - 1, side],
-                z_send.at[j - 1, side],
-                z_recv.at[j - 1, side],
-                (place, lax.rem(level + j, n_shard)),
-            )
-
-    for tick in range(len(chunks) + count - 1):
-        for stage in range(count):
-            chunk = tick - stage
-            if 0 <= chunk < len(chunks):
-                advance(chunk, stage)
-
-    mine = sum(bits[b] * (1 << (b - 1)) for b in range(1, count))
-    keeps = []
-    for side in range(2):
-        chunk = chunks.index((0, side))
-        for j in range(1, n_shard):
-            landed(got_z.at[j - 1, side], z_recv.at[j - 1, side])
-
-        def body(i, carry):
-            at = pl.multiple_of(i * step, 16)
-            total = acc[chunk, mine, pl.ds(at, step), :].astype(jnp.float32)
-            for j in range(1, n_shard):
-                total = total + got_z[j - 1, side, pl.ds(at, step), :].astype(jnp.float32)
-            final[side, pl.ds(at, step), :] = total.astype(jnp.bfloat16)
-            return carry
-
-        lax.fori_loop(0, half // step, body, 0)
-        keep = pltpu.make_async_copy(final.at[side], out.at[place, side], keep_sem.at[side])
-        keep.start()
-        keeps.append(keep)
-        push(
-            final.at[side],
-            out.at[place, side],
-            g_send.at[side, 0],
-            g_recv.at[side, 0],
-            (flipped(place, bits, [orders[side][0]]), level),
-        )
-    for stage in range(1, count + 1):
-        for side in range(2):
-            order = orders[side] + [0]
-            for slot, which in enumerate(subsets(order[: stage - 1])):
-                landed(
-                    out.at[flipped(place, bits, which + [order[stage - 1]]), side],
-                    g_recv.at[side, (1 << (stage - 1)) - 1 + slot],
-                )
-            if stage < count:
-                target = flipped(place, bits, [order[stage]])
-                for slot, which in enumerate(subsets(order[:stage])):
-                    piece = flipped(place, bits, which)
-                    index = (1 << stage) - 1 + slot
-                    push(
-                        final.at[side] if not which else out.at[piece, side],
-                        out.at[piece, side],
-                        g_send.at[side, index],
-                        g_recv.at[side, index],
-                        (target, level),
-                    )
-    for keep in keeps:
-        keep.wait()
-    for copy in started:
-        copy.wait_send()
-
-
-def reduce_grads(n_dp, n_shard, grads):
-    shard_lines, piece, padded = geometry(n_dp, n_shard)
-    half = piece // 2
-    count = n_dp.bit_length() - 1
-    chunks = 2 * n_shard
-    pairs = n_dp // 2
-    got_bits = [
-        pltpu.VMEM((chunks, pairs >> t, half, LANES), jnp.bfloat16) for t in range(1, count)
-    ]
-    return pl.pallas_call(
-        functools.partial(reduce_kernel, n_dp, n_shard, half),
-        out_shape=jax.ShapeDtypeStruct((n_dp, 2, half, LANES), jnp.bfloat16),
-        in_specs=[pl.BlockSpec(memory_space=pltpu.HBM)],
-        out_specs=pl.BlockSpec(memory_space=pltpu.HBM),
-        scratch_shapes=[
-            pltpu.VMEM((chunks, pairs, half, LANES), jnp.bfloat16),
-            pltpu.VMEM((chunks, pairs, half, LANES), jnp.bfloat16),
-            *got_bits,
-            pltpu.VMEM((n_shard - 1, 2, half, LANES), jnp.bfloat16),
-            pltpu.VMEM((2, half, LANES), jnp.bfloat16),
-            pltpu.SemaphoreType.DMA((chunks, pairs)),
-            pltpu.SemaphoreType.DMA((chunks, pairs)),
-            pltpu.SemaphoreType.DMA((chunks, pairs)),
-            pltpu.SemaphoreType.DMA((count - 1, chunks, pairs // 2)),
-            pltpu.SemaphoreType.DMA((count - 1, chunks, pairs // 2)),
-            pltpu.SemaphoreType.DMA((n_shard - 1, 2)),
-            pltpu.SemaphoreType.DMA((n_shard - 1, 2)),
-            pltpu.SemaphoreType.DMA((2, n_dp - 1)),
-            pltpu.SemaphoreType.DMA((2, n_dp - 1)),
-            pltpu.SemaphoreType.DMA((2,)),
-        ],
-        compiler_params=pltpu.CompilerParams(
-            collective_id=2, has_side_effects=True, vmem_limit_bytes=60 << 20
-        ),
-        name="reduce_grads",
-    )(grads.reshape(n_shard, n_dp, 2, half, LANES))
-
-
 RIM = 208
 EXT = 1024
 QB = 128
@@ -677,67 +384,656 @@
     )(bounds, rows, weight, vectors)
 
 
-def attend_back_kernel(bounds, queries, keys, values, attended, grads, lse, query_grad, key_grad, value_grad, bias):
+def wide_plan(n_shard, shard_lines):
+    sizes = [(D, 3 * D), (D, D), (D, FF), (FF, D)]
+    plan = [[] for _ in range(n_shard)]
+    cursor = 0
+    for which, (rows, columns) in enumerate(sizes):
+        width = columns // LANES
+        for s in range(n_shard):
+            begin, stop = s * shard_lines, (s + 1) * shard_lines
+            first = max(0, (begin - cursor) // width)
+            last = min(rows, -(-(stop - cursor) // width))
+            if last > first:
+                plan[s].append((which, first // 128 * 128, last, width, cursor - begin))
+        cursor += rows * width
+    return plan, cursor - (n_shard - 1) * shard_lines
+
+
+def fill_lines(wide, left, right, first, last, width, offset):
+    def product(row, group):
+        return lax.dot_general(
+            left[:, pl.ds(row, 128)],
+            right[:, group * 768 : (group + 1) * 768],
+            (((0,), (0,)), ((), ())),
+            preferred_element_type=jnp.float32,
+        )
+
+    def store(row, count):
+        line = MARGIN + offset + row * width
+        for group in range(width // 6):
+            tile = product(row, group)
+            for c in range(6):
+                wide[pl.ds(line + group * 6 + c, count, stride=width), :] = tile[
+                    :count, c * LANES : (c + 1) * LANES
+                ]
+
+    full = (last - first) // 128
+
+    def block(i, carry):
+        store(pl.multiple_of(first + i * 128, 128), 128)
+        return carry
+
+    if full:
+        lax.fori_loop(0, full, block, 0)
+    row = first + full * 128
+    rest = -(-(last - row) // 8) * 8
+    if rest:
+        store(row, rest)
+
+
+class Links:
+    def __init__(self, n_dp, n_shard):
+        self.n_dp, self.n_shard = n_dp, n_shard
+        self.place = lax.axis_index("dp")
+        self.level = lax.axis_index("shard")
+        self.count, self.orders = bit_list(n_dp)
+        self.bits = bits_of(self.place, self.count)
+        self.sent = []
+
+    def push(self, src, dst, send, recv, target):
+        pltpu.make_async_remote_copy(
+            src_ref=src,
+            dst_ref=dst,
+            send_sem=send,
+            recv_sem=recv,
+            device_id=target,
+            device_id_type=MESH,
+        ).start()
+
+    def note(self, refs, when=None):
+        self.sent.append((refs, when))
+
+    def landed(self, buffer, sem):
+        pltpu.make_async_remote_copy(
+            src_ref=buffer,
+            dst_ref=buffer,
+            send_sem=sem,
+            recv_sem=sem,
+            device_id=self.over(0),
+            device_id_type=MESH,
+        ).wait_recv()
+
+    def over(self, bit):
+        return (flipped(self.place, self.bits, [bit]), self.level)
+
+    def drain(self):
+        for refs, when in self.sent:
+
+            def wait(refs=refs):
+                src, send = refs()
+                pltpu.make_async_remote_copy(
+                    src_ref=src,
+                    dst_ref=src,
+                    send_sem=send,
+                    recv_sem=send,
+                    device_id=self.over(0),
+                    device_id_type=MESH,
+                ).wait_send()
+
+            if when is None:
+                wait()
+            else:
+                pl.when(when)(wait)
+
+
+class PlaneSum:
+    def __init__(self, links, wide, part, bufs):
+        self.links, self.wide, self.part = links, wide, part
+        self.core_got, self.core_send, self.core_recv, self.send_bufs, self.got_bufs, self.bit_send, self.bit_recv = bufs
+        self.lines = self.core_got.shape[-2]
+        self.pairs = links.n_dp // 2
+
+    def rows(self, piece, quarter):
+        return pl.ds(pl.multiple_of(MARGIN + (piece * 4 + quarter) * self.lines, 8), self.lines)
+
+    def begin(self):
+        links = self.links
+        core = links.bits[0]
+        for quarter in range(4):
+            for m in range(self.pairs):
+                src = self.wide.at[self.rows(2 * m + 1 - core, quarter)]
+                send = self.core_send.at[self.part, quarter, m]
+                links.push(
+                    src,
+                    self.core_got.at[self.part, quarter, m],
+                    send,
+                    self.core_recv.at[self.part, quarter, m],
+                    links.over(0),
+                )
+                links.note(
+                    lambda quarter=quarter, m=m: (
+                        self.core_got.at[self.part, quarter, m],
+                        self.core_send.at[self.part, quarter, m],
+                    )
+                )
+
+    def members(self, order, stage, flip):
+        bits = self.links.bits
+        base = sum((bits[b] if b != flip else 1 - bits[b]) * (1 << (b - 1)) for b in order[:stage])
+        return [base + sum(1 << (b - 1) for b in which) for which in subsets(order[stage:])]
+
+    def merge(self, piece, quarter, other, into):
+        step = 112
+        start = MARGIN + (piece * 4 + quarter) * self.lines
+
+        def body(i, carry):
+            at = pl.multiple_of(i * step, 16)
+            rows = pl.ds(pl.multiple_of(start + at, 8), step)
+            total = self.wide[rows, :] + other[pl.ds(at, step), :].astype(jnp.float32)
+            if into is None:
+                self.wide[rows, :] = total
+            else:
+                into[pl.ds(at, step), :] = total.astype(into.dtype)
+            return carry
+
+        lax.fori_loop(0, self.lines // step, body, 0)
+
+    def advance(self, quarter, stage, result=None):
+        links, part = self.links, self.part
+        core = links.bits[0]
+        order = links.orders[quarter % 2]
+
+        def incoming(slot, m):
+            if stage == 0:
+                return self.core_got.at[part, quarter, m], self.core_recv.at[part, quarter, m]
+            return (
+                self.got_bufs[stage - 1].at[part, quarter, slot],
+                self.bit_recv.at[stage - 1, part, quarter, slot],
+            )
+
+        if stage == links.count - 1:
+            (m,) = self.members(order, stage, None)
+            buffer, sem = incoming(0, m)
+            links.landed(buffer, sem)
+            self.merge(2 * m + core, quarter, buffer, result)
+            return
+        flip = order[stage]
+        mine = links.bits[flip]
+        for flipping in (True, False):
+            bit = 1 - mine if flipping else mine
+            for e, m in enumerate(self.members(order, stage + 1, flip if flipping else None)):
+                buffer, sem = incoming(2 * e + bit, m)
+                links.landed(buffer, sem)
+                if flipping:
+                    out = self.send_bufs[stage].at[part, quarter, e]
+                    self.merge(2 * m + core, quarter, buffer, out)
+                    send = self.bit_send.at[stage, part, quarter, e]
+                    links.push(
+                        out,
+                        self.got_bufs[stage].at[part, quarter, e],
+                        send,
+                        self.bit_recv.at[stage, part, quarter, e],
+                        links.over(flip),
+                    )
+                    links.note(
+                        lambda stage=stage, e=e: (
+                            self.send_bufs[stage].at[part, quarter, e],
+                            self.bit_send.at[stage, part, quarter, e],
+                        )
+                    )
+                else:
+                    self.merge(2 * m + core, quarter, buffer, None)
+
+
+def plane_scratch(n_dp, lines, parts):
+    count = n_dp.bit_length() - 1
+    pairs = n_dp // 2
+    half = jnp.bfloat16
+    stages = [pltpu.VMEM((parts, 4, pairs >> t, lines, LANES), half) for t in range(1, count)]
+    return (
+        [
+            pltpu.VMEM((parts, 4, pairs, lines, LANES), jnp.float32),
+            pltpu.SemaphoreType.DMA((parts, 4, pairs)),
+            pltpu.SemaphoreType.DMA((parts, 4, pairs)),
+        ]
+        + stages
+        + stages
+        + [
+            pltpu.SemaphoreType.DMA((count - 1, parts, 4, pairs // 2)),
+            pltpu.SemaphoreType.DMA((count - 1, parts, 4, pairs // 2)),
+        ]
+    )
+
+
+def plane_bufs(n_dp, scratch):
+    count = n_dp.bit_length() - 1
+    k = count - 1
+    used = 3 + 2 * k + 2
+    core_got, core_send, core_recv = scratch[:3]
+    bufs = (core_got, core_send, core_recv, scratch[3 : 3 + k], scratch[3 + k : 3 + 2 * k], *scratch[3 + 2 * k : used])
+    return bufs, scratch[used:]
+
+
+def back_kernel(n_dp, n_shard, lines, *refs):
+    (bounds, feed_two, slope, activated, tangent, *attention) = refs[:11]
+    joined, sums, plane = refs[11:14]
+    bufs, rest = plane_bufs(n_dp, refs[14:])
+    (wide_a, wide_b, queries, keys, values, attended, grads, lse, key_grad, value_grad, bias) = rest[:11]
+    (out_rim, got_rim, padded_rim, load_sem, rim_send, rim_recv, plane_sem) = rest[11:]
+    total_lines = (4 * D * D + 2 * D * FF + 8 * D + FF) // n_shard // LANES
+    links = Links(n_dp, n_shard)
+    place, level = links.place, links.level
+    previous, following = ring(n_dp, n_shard, place, level)
+    targets = [queries, keys, values, attended, grads, lse]
+    loads = [
+        pltpu.make_async_copy(src, dst, load_sem.at[i]) for i, (src, dst) in enumerate(zip(attention, targets))
+    ]
+    for load in loads:
+        load.start()
+    greet(n_dp, n_shard, place, level, links.bits, (previous, following))
+    plan, tail = wide_plan(n_shard, total_lines)
+    lefts = [None, None, feed_two, activated]
+    rights = [None, None, slope, tangent]
+    early = [PlaneSum(links, wide_a, 0, bufs), PlaneSum(links, wide_b, 1, bufs)]
+
+    def fill(wide, entry):
+        which, first, last, width, offset = entry
+        fill_lines(wide, lefts[which], rights[which], first, last, width, offset)
+
+    for entry in plan[n_shard - 1]:
+        fill(wide_a, entry)
+    early[0].begin()
+    second = plan[n_shard - 2]
+    fill(wide_b, second[0])
+    for quarter in range(4):
+        early[0].advance(quarter, 0)
+    for entry in second[1:]:
+        fill(wide_b, entry)
+    early[1].begin()
+    for load in loads:
+        load.wait()
     start = bounds[0, 0]
-    for block in range(BLOCK // QB):
+    live = bounds[0, 1] - bounds[0, 0]
+    blocks = BLOCK // QB
+    for block in range(blocks):
         bias[block] = window_bias(start, block)
     key_grad[...] = jnp.zeros_like(key_grad)
     value_grad[...] = jnp.zeros_like(value_grad)
+    sums[...] = jnp.zeros_like(sums)
+    last_stage = links.count - 1
+    chain = []
+    for part in range(2):
+        for quarter in range(4):
+            for stage in range(1 if part == 0 else 0, last_stage):
+                chain.append((4 + 9 * part + 2.5 * quarter + (stage - 1) * 8 + (3 if part else 0), part, quarter, stage))
+    ticks = {}
+    for when, part, quarter, stage in sorted(chain):
+        ticks.setdefault(min(int(when), 23), []).append((part, quarter, stage))
+
+    def send_rim(pair):
+        for kind, source in enumerate((key_grad, value_grad)):
+            base = pair * EXT
+            out_rim[0, pair, kind] = source[pl.ds(pl.multiple_of(base, EXT), RIM), :].astype(jnp.bfloat16)
+            out_rim[1, pair, kind] = source[pl.ds(base + RIM + live, RIM), :].astype(jnp.bfloat16)
+        for side, target in enumerate((previous, following)):
+            links.push(
+                out_rim.at[side, pair], got_rim.at[side, pair], rim_send.at[side, pair], rim_recv.at[side, pair], target
+            )
 
     def body(i, carry):
-        block = lax.rem(i, BLOCK // QB)
-        pair = lax.div(i, BLOCK // QB)
+        block = lax.rem(i, blocks)
+        pair = lax.div(i, blocks)
         at = pl.multiple_of(block * QB, QB)
         lanes = pl.ds(pl.multiple_of(pair * LANES, LANES), LANES)
         asked = stacked(queries[pl.ds(at, QB), lanes])
-        own_grad = grads[pl.ds(at, QB), lanes]
-        given = stacked(own_grad)
+        given = stacked(grads[pl.ds(at, QB), lanes])
+        near = pl.ds(pl.multiple_of(pair * EXT + at, QB), WIN)
         near_keys = keys[pl.ds(at, WIN), lanes]
         near_values = values[pl.ds(at, WIN), lanes]
         scores = lax.dot_general(
             asked, near_keys, (((1,), (1,)), ((), ())), preferred_element_type=jnp.float32
         )
         cover = bias[block]
-        level = lse[pair, block]
+        height = lse[pair, block]
         probs = jnp.exp(
-            scores + jnp.concatenate([cover, cover], axis=0) - jnp.concatenate([level] * (WIN // LANES), axis=1)
+            scores + jnp.concatenate([cover, cover], axis=0) - jnp.concatenate([height] * (WIN // LANES), axis=1)
         )
         prob_grad = lax.dot_general(
             given, near_values, (((1,), (1,)), ((), ())), preferred_element_type=jnp.float32
         )
-        wide = given.astype(jnp.float32) * jnp.concatenate([attended[pl.ds(at, QB), lanes]] * 2, axis=0).astype(
+        both = given.astype(jnp.float32) * jnp.concatenate([attended[pl.ds(at, QB), lanes]] * 2, axis=0).astype(
             jnp.float32
         )
-        centre = jnp.sum(wide, axis=-1, keepdims=True)
+        centre = jnp.sum(both, axis=-1, keepdims=True)
         score_grad = (probs * (prob_grad - centre)).astype(jnp.bfloat16)
-        query_grad[pl.ds(at, QB), lanes] = (
-            unstacked(jnp.dot(score_grad, near_keys, preferred_element_type=jnp.float32)) * 0.125
-        )
-        key_grad[pl.ds(at, WIN), lanes] += lax.dot_general(
+        query_grad = unstacked(jnp.dot(score_grad, near_keys, preferred_element_type=jnp.float32)) * 0.125
+        joined[pl.ds(at, QB), lanes] = query_grad.astype(jnp.bfloat16)
+        sums[0:1, lanes] += jnp.sum(query_grad, axis=0, keepdims=True)
+        key_grad[near, :] += lax.dot_general(
             score_grad, asked, (((0,), (0,)), ((), ())), preferred_element_type=jnp.float32
         )
-        value_grad[pl.ds(at, WIN), lanes] += lax.dot_general(
+        value_grad[near, :] += lax.dot_general(
             probs.astype(jnp.bfloat16), given, (((0,), (0,)), ((), ())), preferred_element_type=jnp.float32
         )
+
+        @pl.when(block == blocks - 1)
+        def _():
+            send_rim(pair)
+
+        for key, work in ticks.items():
+
+            @pl.when(i == key)
+            def _(work=work):
+                for part, quarter, stage in work:
+                    early[part].advance(quarter, stage)
+
         return carry
 
-    lax.fori_loop(0, HEADS // 2 * (BLOCK // QB), body, 0)
-
-
-def attend_back(bounds, queries, keys, values, attended, grads, lse):
+    lax.fori_loop(0, HEADS // 2 * blocks, body, 0)
+    for side in range(2):
+        for pair in range(HEADS // 2):
+            links.note(lambda side=side, pair=pair: (out_rim.at[side, pair], rim_send.at[side, pair]))
+    spot = place * n_shard + level
+    padded_rim[...] = jnp.zeros_like(padded_rim)
+    chunk = 64
+
+    def settle(pair, carry):
+        links.landed(got_rim.at[0, pair], rim_recv.at[0, pair])
+        links.landed(got_rim.at[1, pair], rim_recv.at[1, pair])
+        at_pair = pl.multiple_of(pair * LANES, LANES)
+        base = pair * EXT
+        for kind, source in enumerate((key_grad, value_grad)):
+            after = got_rim[0, pair, kind].astype(jnp.float32)
+            padded_rim[BLOCK : BLOCK + RIM, :] = jnp.where(spot < n_dp * n_shard - 1, after, 0.0)
+
+            def rows(r, inner):
+                at = pl.multiple_of(r * chunk, chunk)
+                slot = lax.broadcasted_iota(jnp.int32, (chunk, 1), 0) + at
+                own = source[pl.ds(pl.multiple_of(base + RIM + at, 16), chunk), :]
+                own = jnp.where(slot < live, own, 0.0)
+                own = own + padded_rim[pl.ds(BLOCK + RIM - live + at, chunk), :]
+                source[pl.ds(pl.multiple_of(base + RIM + at, 16), chunk), :] = own
+                return inner
+
+            lax.fori_loop(0, BLOCK // chunk, rows, 0)
+            before = got_rim[1, pair, kind].astype(jnp.float32)
+            head = source[pl.ds(pl.multiple_of(base + RIM, 16), RIM), :] + jnp.where(spot > 0, before, 0.0)
+            source[pl.ds(pl.multiple_of(base + RIM, 16), RIM), :] = head
+            own = source[pl.ds(pl.multiple_of(base + RIM, 16), BLOCK), :]
+            joined[:, pl.ds(pl.multiple_of((1 + kind) * D + at_pair, LANES), LANES)] = own.astype(jnp.bfloat16)
+            if kind:
+                sums[1:2, pl.ds(at_pair, LANES)] = jnp.sum(own, axis=0, keepdims=True)
+        return carry
+
+    lax.fori_loop(0, HEADS // 2, settle, 0)
+    for part in range(2):
+        for quarter in range(4):
+            early[part].advance(quarter, last_stage)
+            piece = links.place
+            pltpu.make_async_copy(
+                early[part].wide.at[early[part].rows(piece, quarter)],
+                plane.at[1 - part, quarter],
+                plane_sem.at[part, quarter],
+            ).start()
+    for part in range(2):
+        for quarter in range(4):
+            pltpu.make_async_copy(
+                early[part].wide.at[early[part].rows(links.place, quarter)],
+                plane.at[1 - part, quarter],
+                plane_sem.at[part, quarter],
+            ).wait()
+    links.drain()
+
+
+def back_attention(n_dp, n_shard, bounds, feed_two, slope, activated, tangent, *attention):
+    shard_lines, piece, padded = geometry(n_dp, n_shard)
+    lines = piece // 4
+    half = jnp.bfloat16
+    vmem = pl.BlockSpec(memory_space=pltpu.VMEM)
+    hbm = pl.BlockSpec(memory_space=pltpu.HBM)
+    pairs = HEADS // 2
+    wide = pltpu.VMEM((MARGIN + padded + 128, LANES), jnp.float32)
     return pl.pallas_call(
-        attend_back_kernel,
+        functools.partial(back_kernel, n_dp, n_shard, lines),
         out_shape=[
-            jax.ShapeDtypeStruct((BLOCK, D), jnp.float32),
-            jax.ShapeDtypeStruct((EXT, D), jnp.float32),
-            jax.ShapeDtypeStruct((EXT, D), jnp.float32),
+            jax.ShapeDtypeStruct((BLOCK, 3 * D), half),
+            jax.ShapeDtypeStruct((8, D), jnp.float32),
+            jax.ShapeDtypeStruct((2, 4, lines, LANES), jnp.float32),
         ],
-        in_specs=[pl.BlockSpec(memory_space=pltpu.SMEM)] + [pl.BlockSpec(memory_space=pltpu.VMEM)] * 6,
-        out_specs=[pl.BlockSpec(memory_space=pltpu.VMEM)] * 3,
-        scratch_shapes=[pltpu.VMEM((BLOCK // QB, QB, WIN), jnp.float32)],
-        compiler_params=pltpu.CompilerParams(vmem_limit_bytes=60 << 20),
-        name="attend_back",
-    )(bounds, queries, keys, values, attended, grads, lse)
+        in_specs=[pl.BlockSpec(memory_space=pltpu.SMEM)] + [vmem] * 4 + [hbm] * 6,
+        out_specs=[vmem, vmem, hbm],
+        scratch_shapes=plane_scratch(n_dp, lines, 2)
+        + [wide, wide]
+        + [pltpu.VMEM(a.shape, a.dtype) for a in attention]
+        + [
+            pltpu.VMEM((pairs * EXT, LANES), jnp.float32),
+            pltpu.VMEM((pairs * EXT, LANES), jnp.float32),
+            pltpu.VMEM((BLOCK // QB, QB, WIN), jnp.float32),
+            pltpu.VMEM((2, pairs, 2, RIM, LANES), half),
+            pltpu.VMEM((2, pairs, 2, RIM, LANES), half),
+            pltpu.VMEM((2 * BLOCK + RIM + 64, LANES), jnp.float32),
+            pltpu.SemaphoreType.DMA((6,)),
+            pltpu.SemaphoreType.DMA((2, pairs)),
+            pltpu.SemaphoreType.DMA((2, pairs)),
+            pltpu.SemaphoreType.DMA((2, 4)),
+        ],
+        compiler_params=pltpu.CompilerParams(
+            collective_id=2, has_side_effects=True, vmem_limit_bytes=63 << 20
+        ),
+        name="back_attention",
+    )(bounds, feed_two, slope, activated, tangent, *attention)
+
+
+def finish_kernel(n_dp, n_shard, lines, *refs):
+    (joined, feed_one, attended, middle, feed_two, slope, early_plane, vec) = refs[:8]
+    out, vec_out = refs[8:10]
+    bufs, rest = plane_bufs(n_dp, refs[10:])
+    wide_a, wide_b, plane, z_out, z_got, final, vec_got, vec_work = rest[:8]
+    plane_sem, z_send, z_recv, g_send, g_recv, keep_sem, v_send, v_recv = rest[8:]
+    total_lines = (4 * D * D + 2 * D * FF + 8 * D + FF) // n_shard // LANES
+    links = Links(n_dp, n_shard)
+    place, level, count = links.place, links.level, links.count
+    step = 112
+    plane_load = pltpu.make_async_copy(
+        early_plane, plane.at[pl.ds(n_shard - 2, 2)], plane_sem.at[0]
+    )
+    plane_load.start()
+    greet(n_dp, n_shard, place, level, links.bits)
+    plan, tail = wide_plan(n_shard, total_lines)
+    lefts = [feed_one, attended, feed_two, None]
+    rights = [joined, middle, slope, None]
+    late = [PlaneSum(links, wide_b, 0, bufs), PlaneSum(links, wide_a, 1, bufs)]
+
+    def fill(wide, entry):
+        which, first, last, width, offset = entry
+        fill_lines(wide, lefts[which], rights[which], first, last, width, offset)
+
+    def gathered(parts):
+        def body(i, carry):
+            at = pl.multiple_of(i * step, 16)
+            total = parts[0][pl.ds(at, step), :].astype(jnp.float32)
+            for other in parts[1:-1]:
+                total = total + other[pl.ds(at, step), :].astype(jnp.float32)
+            parts[-1][pl.ds(at, step), :] = total.astype(jnp.bfloat16)
+            return carry
+
+        lax.fori_loop(0, lines // step, body, 0)
+
+    def chain(s, quarter, k):
+        for below in (True, False):
+            actor = k if below else n_shard - 1 - k
+            if (actor >= s) if below else (actor <= s):
+                continue
+            side = 0 if below else 1
+
+            @pl.when(level == actor)
+            def _(side=side, below=below):
+                parts = [plane.at[s, quarter]]
+                if k:
+                    links.landed(z_got.at[s, quarter, side], z_recv.at[s, quarter, side])
+                    parts.append(z_got.at[s, quarter, side])
+                gathered(parts + [z_out.at[s, quarter]])
+                links.push(
+                    z_out.at[s, quarter],
+                    z_got.at[s, quarter, side],
+                    z_send.at[s, quarter],
+                    z_recv.at[s, quarter, side],
+                    (place, level + (1 if below else -1)),
+                )
+
+        if k == max(s, n_shard - 1 - s):
+
+            @pl.when(level == s)
+            def _():
+                parts = [plane.at[s, quarter]]
+                for side, there in ((0, s > 0), (1, s < n_shard - 1)):
+                    if there:
+                        links.landed(z_got.at[s, quarter, side], z_recv.at[s, quarter, side])
+                        parts.append(z_got.at[s, quarter, side])
+                gathered(parts + [final.at[quarter]])
+
+    for s in range(n_shard):
+        for quarter in range(4):
+            links.note(lambda s=s, quarter=quarter: (z_out.at[s, quarter], z_send.at[s, quarter]), level != s)
+
+    def spread(quarter, stage):
+        order = links.orders[quarter % 2] + [0]
+        if stage == 0:
+            pltpu.make_async_copy(final.at[quarter], out.at[place, quarter], keep_sem.at[quarter]).start()
+        else:
+            for slot, which in enumerate(subsets(order[: stage - 1])):
+                piece = flipped(place, links.bits, which + [order[stage - 1]])
+                links.landed(out.at[piece, quarter], g_recv.at[quarter, (1 << (stage - 1)) - 1 + slot])
+        if stage < count:
+            for slot, which in enumerate(subsets(order[:stage])):
+                piece = flipped(place, links.bits, which)
+                index = (1 << stage) - 1 + slot
+                src = final.at[quarter] if not which else out.at[piece, quarter]
+                links.push(
+                    src, out.at[piece, quarter], g_send.at[quarter, index], g_recv.at[quarter, index], links.over(order[stage])
+                )
+                links.note(lambda index=index: (final.at[quarter], g_send.at[quarter, index]))
+
+    def share(stage):
+        if stage == 0:
+            vec_work[0] = vec[...]
+        elif stage <= count:
+            links.landed(vec_got.at[stage - 1], v_recv.at[stage - 1])
+            vec_work[stage] = vec_work[stage - 1] + vec_got[stage - 1]
+        if stage < count:
+            links.push(vec_work.at[stage], vec_got.at[stage], v_send.at[stage], v_recv.at[stage], links.over(stage))
+            links.note(lambda: (vec_work.at[stage], v_send.at[stage]))
+        elif stage == count:
+            for j in range(1, n_shard):
+                links.push(
+                    vec_work.at[count],
+                    vec_got.at[count + j - 1],
+                    v_send.at[count + j - 1],
+                    v_recv.at[count + j - 1],
+                    (place, lax.rem(level + j, n_shard)),
+                )
+                links.note(lambda j=j: (vec_work.at[count], v_send.at[count + j - 1]))
+        else:
+            total = vec_work[count]
+            for j in range(1, n_shard):
+                links.landed(vec_got.at[count + j - 1], v_recv.at[count + j - 1])
+                total = total + vec_got[count + j - 1]
+            vec_out[...] = total
+
+    last_stage = count - 1
+    work = []
+    for quarter in range(4):
+        for k in range(n_shard):
+            work.append((2.5 * quarter + 6 * k, "z", n_shard - 1, quarter, k))
+            work.append((10 + 2.5 * quarter + 6 * k, "z", n_shard - 2, quarter, k))
+            work.append((26.5 + 2.5 * quarter + 4 * k, "z", 1, quarter, k))
+            work.append((39.5 + 2.5 * quarter + 4 * k, "z", 0, quarter, k))
+        for stage in range(count):
+            work.append((12 + 2.5 * quarter + 7 * stage, "p", 0, quarter, stage))
+            work.append((21 + 2.5 * quarter + 9 * stage, "p", 1, quarter, stage))
+        for stage in range(count + 1):
+            work.append((52 + 2.5 * quarter + 4 * stage, "g", 0, quarter, stage))
+    for stage in range(count + 2):
+        work.append((3 + 5 * stage, "v", 0, 0, stage))
+    work.sort()
+
+    def run_until(limit):
+        while work and work[0][0] < limit:
+            when, kind, a, quarter, stage = work.pop(0)
+            if kind == "z":
+                chain(a, quarter, stage)
+            elif kind == "p":
+                late[a].advance(quarter, stage, plane.at[1 - a, quarter] if stage == last_stage else None)
+            elif kind == "g":
+                spread(quarter, stage)
+            else:
+                share(stage)
+
+    fill(wide_b, plan[1][0])
+    plane_load.wait()
+    run_until(4)
+    for entry in plan[1][1:]:
+        fill(wide_b, entry)
+    late[0].begin()
+    run_until(8)
+    for entry in plan[0]:
+        which, first, last, width, offset = entry
+        middle_row = (first + last) // 256 * 128
+        if which == 0 and middle_row > first:
+            fill(wide_a, (which, first, middle_row, width, offset))
+            run_until(13)
+            fill(wide_a, (which, middle_row, last, width, offset))
+        else:
+            fill(wide_a, entry)
+    late[1].begin()
+    run_until(1 << 30)
+    for quarter in range(4):
+        pltpu.make_async_copy(final.at[quarter], out.at[place, quarter], keep_sem.at[quarter]).wait()
+    links.drain()
+
+
+def finish_grads(n_dp, n_shard, *operands):
+    shard_lines, piece, padded = geometry(n_dp, n_shard)
+    lines = piece // 4
+    count = n_dp.bit_length() - 1
+    half = jnp.bfloat16
+    vmem = pl.BlockSpec(memory_space=pltpu.VMEM)
+    hbm = pl.BlockSpec(memory_space=pltpu.HBM)
+    wide = pltpu.VMEM((MARGIN + padded + 128, LANES), jnp.float32)
+    vec = operands[-1].shape
+    return pl.pallas_call(
+        functools.partial(finish_kernel, n_dp, n_shard, lines),
+        out_shape=[
+            jax.ShapeDtypeStruct((n_dp, 4, lines, LANES), half),
+            jax.ShapeDtypeStruct(vec, jnp.float32),
+        ],
+        in_specs=[vmem] * 6 + [hbm, vmem],
+        out_specs=[hbm, vmem],
+        scratch_shapes=plane_scratch(n_dp, lines, 2)
+        + [
+            wide,
+            wide,
+            pltpu.VMEM((n_shard, 4, lines, LANES), jnp.float32),
+            pltpu.VMEM((n_shard, 4, lines, LANES), half),
+            pltpu.VMEM((n_shard, 4, 2, lines, LANES), half),
+            pltpu.VMEM((4, lines, LANES), half),
+            pltpu.VMEM((count + n_shard - 1, *vec), jnp.float32),
+            pltpu.VMEM((count + 1, *vec), jnp.float32),
+            pltpu.SemaphoreType.DMA((1,)),
+            pltpu.SemaphoreType.DMA((n_shard, 4)),
+            pltpu.SemaphoreType.DMA((n_shard, 4, 2)),
+            pltpu.SemaphoreType.DMA((4, n_dp - 1)),
+            pltpu.SemaphoreType.DMA((4, n_dp - 1)),
+            pltpu.SemaphoreType.DMA((4,)),
+            pltpu.SemaphoreType.DMA((count + n_shard - 1,)),
+            pltpu.SemaphoreType.DMA((count + n_shard - 1,)),
+        ],
+        compiler_params=pltpu.CompilerParams(
+            collective_id=3, has_side_effects=True, vmem_limit_bytes=63 << 20
+        ),
+        name="finish_grads",
+    )(*operands)
 
 
 def gelu_value(preact):
@@ -830,29 +1126,22 @@
     attended_grad = jnp.einsum(
         "te,de->td", middle_feed, weight_out, preferred_element_type=jnp.float32
     ).astype(jnp.bfloat16)
-    query_grads, key_ext, value_ext = attend_back(
-        token_bounds, queries, keys, values, attended_list, attended_grad, lse
-    )
-    ext_grad = jnp.concatenate([key_ext, value_ext], axis=1)
-    device_count = n_dp * n_shard
-    forward = [(i, (i + 1) % device_count) for i in range(device_count)]
-    backward = [((i + 1) % device_count, i) for i in range(device_count)]
-    from_after = lax.ppermute(ext_grad[:RIM], ("dp", "shard"), backward)
-    from_before = lax.ppermute(
-        lax.dynamic_slice_in_dim(ext_grad, RIM + live_count, RIM, 0), ("dp", "shard"), forward
-    )
-    spot = lax.axis_index(("dp", "shard"))
-    from_before = jnp.where((spot > 0), from_before, 0.0)
-    from_after = jnp.where((spot < device_count - 1), from_after, 0.0)
-    own_grad = jnp.where(is_live[:, None], ext_grad[RIM : RIM + BLOCK], 0.0)
-    own_grad = own_grad.at[:RIM].add(from_before)
-    own_grad = jnp.pad(own_grad, ((16, 0), (0, 0)))
-    at = live_count + 16 - RIM
-    tail_now = lax.dynamic_slice_in_dim(own_grad, at, RIM, 0)
-    own_grad = lax.dynamic_update_slice_in_dim(own_grad, tail_now + from_after, at, 0)[16:]
-    grad_bias_q = jnp.sum(query_grads, axis=0)
-    grad_bias_v = jnp.sum(own_grad[:, D:], axis=0)
-    joined = jnp.concatenate([query_grads, own_grad], axis=1).astype(jnp.bfloat16)
+    joined, sums, plane = back_attention(
+        n_dp,
+        n_shard,
+        token_bounds,
+        second_feed,
+        slope_feed,
+        activated,
+        tangent_b,
+        queries,
+        keys,
+        values,
+        attended_list,
+        attended_grad,
+        lse,
+    )
+    grad_bias_q, grad_bias_v = sums[0], sums[1]
     back_one = jnp.einsum("te,de->td", joined, weight_qkv, preferred_element_type=jnp.float32)
     grad_gain_one = jnp.sum(back_one * first_normed, axis=0)
     grad_shift_one = jnp.sum(back_one, axis=0)
@@ -871,22 +1160,24 @@
         ]
     )
     vector_lines = jnp.concatenate([vector_grad.reshape(-1), grad_bias_in]).reshape(-1, LANES)
-    flat_grads = weight_grads(
+    reduced, vector_sum = finish_grads(
         n_dp,
         n_shard,
+        joined,
         first_feed,
-        joined,
         attended_list,
         middle_feed,
         second_feed,
         slope_feed,
-        activated,
-        tangent_b,
+        plane,
         vector_lines,
     )
-    reduced = reduce_grads(n_dp, n_shard, flat_grads).reshape(-1)
+    reduced = reduced.reshape(-1)
     piece_len = own_len // n_dp
     grad_shard = reduced[:own_len].astype(jnp.float32)
+    vector_len = 8 * D + FF
+    with_vectors = jnp.concatenate([grad_shard[: own_len - vector_len], vector_sum.reshape(-1)])
+    grad_shard = jnp.where(lax.axis_index("shard") == n_shard - 1, with_vectors, grad_shard)
     grad_piece = lax.dynamic_slice_in_dim(
         grad_shard, lax.axis_index("dp") * piece_len, piece_len, 0
     )

time: 449 us -> 388 us (0.86)
  waiting for transfers between devices: 61.2 us -> 0 us
  Pallas kernels: 284 us -> 297 us
  local copies, waits for them, and re-layouts: 36.6 us -> 28 us
  starting transfers between devices: 4.89 us -> 0 us
    ppermute x2 -> x0, waiting for transfers between devices: 61.2 us -> none  [the longest x1 61.2 us: shards(): lax.ppermute(lax.dynamic_slice_in_dim(ext_grad, RIM + live_count, RIM, 0)...]
    pallas_call x3 -> x2, Pallas kernels: 146 us -> 158 us  [the longest x1 83.9 us: finish_grads(): pl.pallas_call(functools.partial(finish_kernel, n_dp, n_shard, lines), ou...]
    unnamed x51 -> x40, local copies, waits for them, and re-layouts: 10 us -> 3.81 us
    sub x1, other arithmetic: 14.7 us -> 20.8 us  [shards(): params - learn_rate * (first_hat / (jnp.sqrt(second_hat) + adam_eps) + de...]
    ppermute x2 -> x0, starting transfers between devices: 4.89 us -> none  [the longest x1 4.89 us: shards(): from_after = lax.ppermute(ext_grad[:RIM], ('dp', 'shard'), backward)]
  transfers between devices with their start and end apart: 2 -> 0, of which waited for: 1 -> 0; matrix products, arithmetic and copies ran while one was open for 2% -> 0% of each run, Pallas kernels for 0% -> 0%
where the time goes in v3:
time: 388 us; the launch traced here: 387 us
  Pallas kernels  297 us (77%)
  other arithmetic  35.1 us (9%)
  local copies, waits for them, and re-layouts  28 us (7%)
  matrix products  24.4 us (6%)
    pallas_call x1, Pallas kernels, gather_weights(): pl.pallas_call(functools.partial(gather_kernel, n_dp, n_shard, half), out...  92.2 us
    pallas_call x1, Pallas kernels, finish_grads(): pl.pallas_call(functools.partial(finish_kernel, n_dp, n_shard, lines), ou...  83.9 us
    pallas_call x1, Pallas kernels, back_attention(): pl.pallas_call(functools.partial(back_kernel, n_dp, n_shard, lines), out_...  73.9 us
    pallas_call x1, Pallas kernels, attend(): pl.pallas_call(attend_kernel, out_shape=[jax.ShapeDtypeStruct((BLOCK, D),...  30.4 us
    sub x1, other arithmetic, shards(): params - learn_rate * (first_hat / (jnp.sqrt(second_hat) + adam_eps) + de...  20.8 us
    pallas_call x1, Pallas kernels, lay_out_weights(): pl.pallas_call(functools.partial(layout_kernel, n_shard, shard_lines, pad...  16.8 us

profile of v3, /device:TPU:1, one launch (start us, length us, event | category | flops | bytes accessed | tf_op | source)
XLA Modules:
  0.0 387.1 jit_solution(6000234771008915674)
XLA Ops:
  0.6 0.0 copy-start.10
  0.7 0.1 pad.16.clone
  0.7 1.3 fusion.22
  3.4 1.3 convert_reduce_fusion
  4.7 1.5 fusion.17
  6.2 2.0 pad_dynamic-slice_fusion
  8.2 0.0 copy-done.10
  8.2 0.3 convert_reduce_fusion.1
  8.4 0.0 copy-start.6
  8.5 3.5 convert_element_type.33
  12.0 4.0 %pad_bitcast_fusion = (bf16[14336,128]{1,0:T(8,128)(2,1)}, bf16[1835008]{0:T(1024)(128)(2,1)}) fusion(bf16[1771776]{0:T(1024)(128)(2,1)S(1)} %convert_element_type.33), kind=kLoop, calls=%fused_computation.61 | loop fusion | bytes 10883584 | tf_op jit(solution)/shard_map/reshape;reshape | solution.py:270
  16.0 92.2 %gather_weights.1 = (bf16[4,8,2,896,128]{4,3,2,1,0:T(8,128)(2,1)}, bf16[208,768]{1,0:T(8,128)(2,1)}, bf16[208,768]{1,0:T(8,128)(2,1)}) custom-call(bf16[8,2,896,128]{3,2,1,0:T(8,128)(2,1)} %bitcast.38, bf16[208,768]{1,0:T(8,128)(2,1)} %get-tuple-element.65.head, bf16[208,768]{1,0:T(8,128)(2,1)} %get-tuple-element.64.tail), custom_call_target="tpu_custom_call" | custom-call | tf_op jit(solution)/shard_map/gather_weights/pallas_call | solution.py:167
  108.2 0.0 copy-done
  108.2 1.2 maximum_maximum_fusion
  109.4 2.9 dynamic_update_slice.3.rows
  112.3 0.0 copy-start.7
  112.3 16.8 %lay_out_weights.1 = (bf16[768,2304]{1,0:T(8,128)(2,1)}, bf16[768,768]{1,0:T(8,128)(2,1)}, bf16[768,3072]{1,0:T(8,128)(2,1)}, bf16[3072,768]{1,0:T(8,128)(2,1)}, f32[72,128]{1,0:T(8,128)}) custom-call(bf16[14336,128]{1,0:T(8,128)(2,1)} %get-tuple-element.62.own, bf16[4,14336,128]{2,1,0:T(8,128)(2,1)} %bitcast.37), custom_call_target="tpu_custom_call" | custom-call | tf_op jit(solution)/shard_map/lay_out_weights/pallas_call | solution.py:257
  129.2 0.0 copy-done.7
  129.2 0.0 copy-start.12
  129.2 0.8 slice_bitcast_fusion
  130.0 0.8 slice_bitcast_fusion.1
  130.8 0.7 slice.54
  131.5 0.6 reshape.94.vectors
  132.1 30.4 %attend.1 = (bf16[512,768]{1,0:T(8,128)(2,1)}, bf16[512,768]{1,0:T(8,128)(2,1)}, bf16[1024,768]{1,0:T(8,128)(2,1)}, bf16[1024,768]{1,0:T(8,128)(2,1)}, bf16[512,...) custom-call(s32[1,2]{1,0:T(1,128)} %refs_0_.1, bf16[1024,768]{1,0:T(8,128)(2,1)} %copy-done.7, ...), custom_call_target="tpu_custom_call" | custom-call | tf_op jit(solution)/shard_map/attend/pallas_call | solution.py:366
  162.5 0.0 copy-done.12
  162.5 0.0 slice-start.3
  162.5 2.2 fusion.23
  164.7 0.3 multiply_reduce_fusion.2
  165.0 0.0 slice-start.4
  165.0 0.3 add_convert_fusion.refs_1_.refs_4_
  165.4 0.0 slice-start.5
  165.4 3.7 multiply_convert_fusion
  169.0 0.0 copy-done.5
  169.1 0.0 copy-start.8
  169.1 0.0 slice-done.4
  169.1 0.0 slice-done.5
  169.1 4.9 %fusion.21 = (f32[3072]{0:T(1024)S(1)}, bf16[512,3072]{1,0:T(8,128)(2,1)S(1)}) fusion(f32[512,3072]{1,0:T(8,128)S(1)} %get-tuple-element.76, f32[3072]{0:T(1024)S(1)} %slice_bitcast_fusion, bf16[512,768]{1,0:T(8,128)(2,1)S(1)} %get-tuple-element.57.refs_4_, bf16[3072,768]{1,0:T(8,128)(2,1)S(1)} %bitcast.45), kind=kOutput, calls=%fused_computation.63 | convolution fusion | flops 2434790400 | bytes 14966784 | tf_op jit(solution)/shard_map/td,fd->tf/dot_general | solution.py:1115
  174.0 0.0 copy-start.4
  174.0 3.8 add_select_fusion
  177.8 0.0 copy-done.4
  177.8 3.1 multiply_reduce_fusion
  180.9 0.6 fusion.20
  181.5 0.0 copy-start.1
  181.5 1.1 copy-done.1
  182.7 0.1 convert_element_type.38.refs_3_
  182.8 0.9 copy-done.9
  183.7 1.7 convolution_convert_fusion.refs_9_
  185.4 73.9 %back_attention.1 = (bf16[512,2304]{1,0:T(8,128)(2,1)}, f32[8,768]{1,0:T(8,128)}, f32[2,4,448,128]{3,2,1,0:T(8,128)}) custom-call(s32[1,2]{1,0:T(1,128)} %refs_0_.1, bf16[512,768]{1,0:T(8,128)(2,1)} %copy-done.5, bf16[512,3072]{1,0:T(8,128)(2,1)} %copy-done.4, bf16[512,3072]{1,0:T(8,128)(2,1)} %copy-done.8, bf16[512,768]{1,0:T(8,128)(2,1)} %copy-done.6, ...), custom_call_target="tpu_custom_call" | custom-call | tf_op jit(solution)/shard_map/back_attention/pallas_call | solution.py:797
  259.3 0.0 copy-start.2
  259.3 5.2 %fusion.16 = (f32[768]{0:T(1024)S(1)}, f32[512]{0:T(512)S(1)}, f32[512]{0:T(512)S(1)}, f32[768]{0:T(1024)S(1)}, f32[512,768]{1,0:T(8,128)S(1)}) fusion(bf16[512,768]{1,0:T(8,128)(2,1)S(1)} %copy-done, f32[512]{0:T(512)S(1)} %add_rsqrt_fusion, f32[512]{0:T(512)S(1)} %broadcast_multiply_fusion.2, f32[768]{0:T(1024)S(1)} %get-tuple-element.66, ...), kind=kOutput, calls=%fused_computation.30 | convolution fusion | flops 1815868928 | bytes 8274944 | tf_op jit(solution)/shard_map/te,de->td/dot_general | solution.py:1145
  264.5 1.7 fusion.15
  266.3 0.7 slice.61
  267.1 0.6 maximum_bitcast_fusion.refs_7_
  267.7 83.9 %finish_grads.1 = (bf16[8,4,448,128]{3,2,1,0:T(8,128)(2,1)}, f32[72,128]{1,0:T(8,128)}) custom-call(bf16[512,2304]{1,0:T(8,128)(2,1)} %get-tuple-element.38.refs_0_, bf16[512,768]{1,0:T(8,128)(2,1)} %get-tuple-element.39.refs_1_, bf16[512,768]{1,0:T(8,128)(2,1)} %get-tuple-element.30.refs_8_.refs_2_, bf16[512,768]{1,0:T(8,128)(2,1)} %copy-done.9, ...), custom_call_target="tpu_custom_call" | custom-call | tf_op jit(solution)/shard_map/finish_grads/pallas_call | solution.py:1005
  351.6 0.0 slice-start
  351.6 2.7 slice_convert_fusion
  354.3 0.0 slice-start.1
  354.3 0.0 copy-start.3
  354.3 0.0 copy-start.11
  354.4 3.8 slice.65
  358.2 1.7 copy-done.3
  359.9 20.8 %multiply_subtract_fusion = (f32[1771776]{0:T(1024)}, f32[1771776]{0:T(1024)}, f32[1771776]{0:T(1024)}, f32[1771776]{0:T(1024)}) fusion(f32[1771776]{0:T(1024)S(1)} %bitcast.36, s32[]{:T(128)S(6)} %mul.214, f32[1771776]{0:T(1024)} %param.10, f32[1771776]{0:T(1024)} %param.11, bf16[1835008]{0:T(1024)(128)(2,1)S(1)} %bitcast.40, f32[9216]{0:T(1024)S(1)} %bitcast.41, ...), kind=kLoop, calls=%fused_computation.4 | loop fusion | flops 37207296 | bytes 60240388 | tf_op jit(solution)/shard_map/sub | solution.py:1191
  380.7 1.5 dynamic_slice.7
  382.2 4.9 %reshape.99 = f32[1,1,221472]{2,1,0:T(1,128)} reshape(f32[221472]{0:T(1024)S(1)} %dynamic_slice.7) | data formatting | bytes 1771776 | tf_op jit(solution)/shard_map/reshape | solution.py:1194
  (34 shorter events, 0.2 us)
Async XLA Ops:
  0.6 7.5 %copy-start.10 = (bf16[512,768]{1,0:T(8,128)(2,1)S(1)}, bf16[512,768]{1,0:T(8,128)(2,1)}, u32[]{:S(2)}) copy-start(bf16[512,768]{1,0:T(8,128)(2,1)} %param.7) | copy-start | bytes 2359300
  8.4 172.4 %copy-start.6 = (bf16[512,768]{1,0:T(8,128)(2,1)}, bf16[512,768]{1,0:T(8,128)(2,1)S(1)}, u32[]{:S(2)}) copy-start(bf16[512,768]{1,0:T(8,128)(2,1)S(1)} %get-tuple-element.57.refs_4_) | copy-start | bytes 2359300
  16.0 92.2 %copy-start = (bf16[512,768]{1,0:T(8,128)(2,1)S(1)}, bf16[512,768]{1,0:T(8,128)(2,1)}, u32[]{:S(2)}) copy-start(bf16[512,768]{1,0:T(8,128)(2,1)} %param.6) | copy-start | bytes 2359300
  112.3 16.8 %copy-start.7 = (bf16[1024,768]{1,0:T(8,128)(2,1)}, bf16[1024,768]{1,0:T(8,128)(2,1)S(1)}, u32[]{:S(2)}) copy-start(bf16[1024,768]{1,0:T(8,128)(2,1)S(1)} %dynamic_update_slice.3.rows) | copy-start | bytes 4718596
  129.2 33.3 %copy-start.12 = (bf16[768,768]{1,0:T(8,128)(2,1)S(1)}, bf16[768,768]{1,0:T(8,128)(2,1)}, u32[]{:S(2)}) copy-start(bf16[768,768]{1,0:T(8,128)(2,1)} %get-tuple-element.31) | copy-start | bytes 3538948
  162.5 2.9 slice-start.2
  162.5 2.9 slice-start.3
  165.0 4.1 %slice-start.4 = ((s8[4718592]{0:T(1024)(128)(4,1)}), s8[4194304]{0:T(1024)(128)(4,1)S(1)}, s32[]{:S(2)}) async-start(s8[4718592]{0:T(1024)(128)(4,1)} %bitcast.44), calls=%async_computation.4 | async-start | bytes 8388608
  165.4 3.7 copy-start.5
  165.4 3.7 slice-start.5
  169.1 4.9 %copy-start.8 = (bf16[512,3072]{1,0:T(8,128)(2,1)}, bf16[512,3072]{1,0:T(8,128)(2,1)S(1)}, u32[]{:S(2)}) copy-start(bf16[512,3072]{1,0:T(8,128)(2,1)S(1)} %get-tuple-element.75.refs_3_) | copy-start | bytes 9437188
  174.0 3.8 copy-start.4
  180.9 2.8 copy-start.13
  181.5 1.1 copy-start.1
  182.8 0.9 copy-start.9
  259.3 5.2 %copy-start.2 = (f32[512,768]{1,0:T(8,128)S(1)}, f32[512,768]{1,0:T(8,128)}, u32[]{:S(2)}) copy-start(f32[512,768]{1,0:T(8,128)} %copy-done.1) | copy-start | bytes 4718596
  351.6 6.6 %slice-start = ((s8[7090176]{0:T(1024)(128)(4,1)}), s8[4194304]{0:T(1024)(128)(4,1)S(1)}, s32[]{:S(2)}) async-start(s8[7090176]{0:T(1024)(128)(4,1)} %bitcast.35), calls=%async_computation | async-start | bytes 8388608
  354.3 3.9 %slice-start.1 = ((s8[7090176]{0:T(1024)(128)(4,1)}), s8[2895872]{0:T(1024)(128)(4,1)S(1)}, s32[]{:S(2)}) async-start(s8[7090176]{0:T(1024)(128)(4,1)} %bitcast.35), calls=%async_computation.1 | async-start | bytes 5791744
  354.3 5.5 %copy-start.3 = (bf16[8,4,448,128]{3,2,1,0:T(8,128)(2,1)S(1)}, bf16[8,4,448,128]{3,2,1,0:T(8,128)(2,1)}, u32[]{:S(2)}) copy-start(bf16[8,4,448,128]{3,2,1,0:T(8,128)(2,1)} %get-tuple-element.42) | copy-start | bytes 11010052
  354.3 5.5 %copy-start.11 = (f32[72,128]{1,0:T(8,128)S(1)}, f32[72,128]{1,0:T(8,128)}, u32[]{:S(2)}) copy-start(f32[72,128]{1,0:T(8,128)} %get-tuple-element.43) | copy-start | bytes 110596
